TPU v7x, 32 devices: a whole 2x2x4 slice. The times are simulated.
32 devices in a mesh: dp: 2 (over x), tp: 16 (over y, z, core).
Axes of the slice: x: 2, y: 2, z: 4, core: 2. Of those that a mesh axis runs over, the one named last changes fastest.
Arguments:
- x: bfloat16 [7168, 5120], P(('dp', 'tp')), parts along dimension 0
- dy: bfloat16 [7168, 5120], P(('dp', 'tp')), parts along dimension 0
- gate: bfloat16 [7168, 16384], P('dp', 'tp'), parts along dimension 0
- up: bfloat16 [7168, 16384], P('dp', 'tp'), parts along dimension 0
- w_gate: bfloat16 [5120, 16384], P(None, 'tp')
- w_up: bfloat16 [5120, 16384], P(None, 'tp')
- w_down: bfloat16 [16384, 5120], P('tp')
Outputs:
- output 1: bfloat16 [7168, 5120], P(('dp', 'tp')), parts along dimension 0
- output 2: bfloat16 [10240, 16384], P('dp', 'tp'), parts along dimension 0
- output 3: bfloat16 [10240, 16384], P('dp', 'tp'), parts along dimension 0
- output 4: bfloat16 [32768, 5120], P(('dp', 'tp')), parts along dimension 0
There are 2 independent parts. A program takes and returns all parts, laid end to end along the dimension named above; an argument that names none is the same for every part.
All inputs are finite; a program needn't handle non-finite values.
Results may differ from a plain program's by a relative error of at most 0.012.
Values are sent between devices in bfloat16 or wider.
A program may use at most 2 GiB of HBM per device.

v0:
```python
import jax
import jax.numpy as jnp


def act(gate, up):
    return jax.nn.silu(gate) * up


def solution(mesh):
    def step(x, dy, gate, up, w_gate, w_up, w_down):
        hidden, back = jax.vjp(act, gate.astype(jnp.float32), up.astype(jnp.float32))
        d_hidden = jnp.dot(dy, w_down.T, preferred_element_type=jnp.float32)
        d_gate, d_up = (g.astype(jnp.bfloat16) for g in back(d_hidden))
        dx = jnp.dot(d_gate, w_gate.T) + jnp.dot(d_up, w_up.T)
        groups = mesh.shape["dp"]

        def by_group(a, b):
            a, b = (t.reshape(groups, -1, t.shape[-1]) for t in (a, b))
            product = jnp.einsum("gta,gtb->gab", a, b, preferred_element_type=jnp.float32)
            return product.astype(jnp.bfloat16).reshape(-1, b.shape[-1])

        return dx, by_group(x, d_gate), by_group(x, d_up), by_group(hidden.astype(jnp.bfloat16), dy)

    return step
```

profile of v0, /device:TPU:0, one launch (start us, length us, event | category | flops | bytes accessed | tf_op | source)
XLA Modules:
  0.0 1111.8 jit_solution(391401981083124588)
XLA Ops:
  7.2 3.2 copy.15
  10.5 0.7 all-gather.11.cloned.1.call-update
  11.2 184.9 %all-gather.9.cloned.1.call-done = bf16[3584,5120]{1,0:T(8,128)(2,1)} async-done(((bf16[224,5120]{1,0:T(8,128)(2,1)}), bf16[3584,5120]{1,0:T(8,128)(2,1)}) %all-gather.9.cloned.1.call-update) | async-done | bytes 36700176 | tf_op args[1]
  196.1 47.1 %fusion.23 = f32[3584,1024]{1,0:T(8,128)} fusion(bf16[3584,5120]{1,0:T(8,128)(2,1)} %all-gather.9.cloned.1.call-done, bf16[1024,5120]{1,0:T(8,128)(2,1)} %param.3), kind=kOutput, calls=%fused_computation.40 | convolution fusion | flops 37580963840 | bytes 61865984 | tf_op jit(solution)/dot_general | solution.py:12
  243.2 17.0 %fusion.22 = (bf16[1,3584,1024]{2,1,0:T(8,128)(2,1)}, bf16[3584,1024]{1,0:T(8,128)(2,1)}) fusion(bf16[3584,1024]{1,0:T(8,128)(2,1)} %param.4, bf16[3584,1024]{1,0:T(8,128)(2,1)} %param.5, f32[3584,1024]{1,0:T(8,128)} %fusion.23), kind=kLoop, calls=%fused_computation.39 | loop fusion | flops 58720256 | bytes 44040192 | tf_op jit(solution)/reshape | solution.py:18
  260.3 46.9 %fusion.24 = bf16[3584,5120]{1,0:T(8,128)(2,1)} fusion(bf16[3584,1024]{1,0:T(8,128)(2,1)} %get-tuple-element.40, bf16[5120,1024]{1,0:T(8,128)(2,1)} %param.6), kind=kOutput, calls=%fused_computation.41 | convolution fusion | flops 37580963840 | bytes 54525952 | tf_op jit(solution)/dot_general | solution.py:14
  307.1 79.0 %convolution_add_fusion = bf16[3584,5120]{1,0:T(8,128)(2,1)} fusion(bf16[3584,5120]{1,0:T(8,128)(2,1)} %fusion.24, bf16[5120,1024]{1,0:T(8,128)(2,1)} %param.7, f32[3584,1024]{1,0:T(8,128)} %fusion.23, bf16[3584,1024]{1,0:T(8,128)(2,1)} %param.5), kind=kOutput, calls=%fused_computation.21 | convolution fusion | flops 37625004032 | bytes 105906176 | tf_op jit(solution)/dot_general | solution.py:14
  386.2 1.6 copy-done
  387.8 0.2 collective-permute-start.4
  388.1 56.5 %convert_bitcast_fusion = bf16[5120,1024]{0,1:T(8,128)(2,1)} fusion(bf16[3584,5120]{1,0:T(8,128)(2,1)} %all-gather.11.cloned.1.call-done, f32[3584,1024]{1,0:T(8,128)} %fusion.23, bf16[3584,1024]{1,0:T(8,128)(2,1)} %param.5), kind=kOutput, calls=%fused_computation.36 | convolution fusion | flops 37611896832 | bytes 69206016 | tf_op jit(solution)/gta,gtb->gab/dot_general | solution.py:19
  444.6 46.6 %convert_bitcast_fusion.1 = bf16[5120,1024]{0,1:T(8,128)(2,1)} fusion(bf16[3584,1024]{1,0:T(8,128)(2,1)} %get-tuple-element.40, bf16[3584,5120]{1,0:T(8,128)(2,1)} %all-gather.11.cloned.1.call-done), kind=kOutput, calls=%fused_computation.37 | convolution fusion | flops 37586206720 | bytes 54525952 | tf_op jit(solution)/gta,gtb->gab/dot_general | solution.py:19
  491.2 14.4 %copy = bf16[5120,1024]{1,0:T(8,128)(2,1)} copy(bf16[5120,1024]{0,1:T(8,128)(2,1)} %convert_bitcast_fusion.1) | data formatting | bytes 20971520
  505.6 14.4 %copy.1 = bf16[5120,1024]{1,0:T(8,128)(2,1)} copy(bf16[5120,1024]{0,1:T(8,128)(2,1)} %convert_bitcast_fusion) | data formatting | bytes 20971520
  520.0 572.8 %while.2 = (bf16[1,3584,1024]{2,1,0:T(8,128)(2,1)}, bf16[1,1,224,5120]{3,2,1,0:T(8,128)(2,1)S(1)}, f32[1,1024,5120]{2,1,0:T(8,128)}, bf16[1,1,224,5120]{3,2,1,0:...) while((bf16[1,3584,1024]{2,1,0:T(8,128)(2,1)}, ...), condition=%wide.windowed_dot_general_cond_ag.clone, body=%wide.windowed_dot_general_body_ag.clone.sunk | while | flops 9419227136 | bytes 144441904 | solution.py:19
  520.2 4.2 collective-permute-start
  524.4 0.6 dynamic-slice.65
  527.0 11.5 %fusion.39 = f32[1024,5120,1]{1,0,2:T(8,128)} fusion(bf16[1,1,224,5120]{3,2,1,0:T(8,128)(2,1)} %get-tuple-element.86, bf16[1,1,224,5120]{3,2,1,0:T(8,128)(2,1)S(1)} %get-tuple-element.84, s32[]{:T(128)S(6)} %multiply.15, bf16[1,1,3584,1024]{3,2,1,0:T(8,128)(2,1)} %bitcast.65, s32[]{:T(128)S(6)} %multiply.16), kind=kOutput, calls=%fused_computation.7.clone.1 | convolution fusion | flops 4701749248 | bytes 32899080 | tf_op jit(solution)/gta,gtb->gab/dot_general | solution.py:19
  538.5 84.8 %collective-permute-done = bf16[1,1,224,5120]{3,2,1,0:T(8,128)(2,1)} collective-permute-done((bf16[1,1,224,5120]{3,2,1,0:T(8,128)(2,1)S(1)}, bf16[1,1,224,5120]{3,2,1,0:T(8,128)(2,1)}, u32[]{:S(2)}, u32[]{:S(2)}) %collective-permute-start) | collective-permute-done | bytes 2293792 | tf_op jit(solution)/gta,gtb->gab/dot_general | solution.py:19
  623.2 4.6 collective-permute-start.1
  627.9 20.8 %collective-permute-start.3 = (bf16[1,1,224,5120]{3,2,1,0:T(8,128)(2,1)}, bf16[1,1,224,5120]{3,2,1,0:T(8,128)(2,1)}, u32[]{:S(2)}, u32[]{:S(2)}) collective-permute-start(bf16[1,1,224,5120]{3,2,1,0:T(8,128)(2,1)} %collective-permute-done.2), channel_id=13, source_target_pairs={{0,1},{1,2},{2,3},{3,4},{4,5},{5,6},{6,7},{7,8},{8,9},{9,10},{10,1... | collective-permute-start | bytes 6881288 | tf_op jit(solution)/gta,gtb->gab/dot_general | solution.py:19
  648.7 19.4 %bitcast_add_fusion.3 = f32[1,1024,5120]{2,1,0:T(8,128)} fusion(f32[1024,5120,1]{1,0,2:T(8,128)} %fusion.39, f32[1,1024,5120]{2,1,0:T(8,128)} %get-tuple-element.85, pred[]{:T(512)S(6)} %compare.6, bf16[1,1,224,5120]{3,2,1,0:T(8,128)(2,1)} %collective-permute-done.2, bf16[1,1,224,5120]{3,2,1,0:T(8,128)(2,1)} %collective-permute-done, ...), kind=kOutput, calls=%fused_computation.clone.1 | convolution fusion | flops 4717477888 | bytes 74842120 | tf_op jit(solution)/gta,gtb->gab/dot_general | solution.py:19
  668.0 15.8 %collective-permute-done.1 = bf16[1,1,224,5120]{3,2,1,0:T(8,128)(2,1)S(1)} collective-permute-done((bf16[1,1,224,5120]{3,2,1,0:T(8,128)(2,1)}, bf16[1,1,224,5120]{3,2,1,0:T(8,128)(2,1)S(1)}, u32[]{:S(2)}, u32[]{:S(2)}) %collective-permute-start.1) | collective-permute-done | bytes 2293792 | tf_op jit(solution)/gta,gtb->gab/dot_general | solution.py:19
  683.9 13.0 %collective-permute-done.3 = bf16[1,1,224,5120]{3,2,1,0:T(8,128)(2,1)} collective-permute-done((bf16[1,1,224,5120]{3,2,1,0:T(8,128)(2,1)}, bf16[1,1,224,5120]{3,2,1,0:T(8,128)(2,1)}, u32[]{:S(2)}, u32[]{:S(2)}) %collective-permute-start.3) | collective-permute-done | bytes 2293792 | tf_op jit(solution)/gta,gtb->gab/dot_general | solution.py:19
  696.8 0.5 collective-permute-start.2
  697.3 0.6 dynamic-slice.65
  699.9 11.5 %fusion.39 = f32[1024,5120,1]{1,0,2:T(8,128)} fusion(bf16[1,1,224,5120]{3,2,1,0:T(8,128)(2,1)} %get-tuple-element.86, bf16[1,1,224,5120]{3,2,1,0:T(8,128)(2,1)S(1)} %get-tuple-element.84, s32[]{:T(128)S(6)} %multiply.15, bf16[1,1,3584,1024]{3,2,1,0:T(8,128)(2,1)} %bitcast.65, s32[]{:T(128)S(6)} %multiply.16), kind=kOutput, calls=%fused_computation.7.clone.1 | convolution fusion | flops 4701749248 | bytes 32899080 | tf_op jit(solution)/gta,gtb->gab/dot_general | solution.py:19
  711.4 34.8 %collective-permute-done = bf16[1,1,224,5120]{3,2,1,0:T(8,128)(2,1)} collective-permute-done((bf16[1,1,224,5120]{3,2,1,0:T(8,128)(2,1)S(1)}, bf16[1,1,224,5120]{3,2,1,0:T(8,128)(2,1)}, u32[]{:S(2)}, u32[]{:S(2)}) %collective-permute-start) | collective-permute-done | bytes 2293792 | tf_op jit(solution)/gta,gtb->gab/dot_general | solution.py:19
  746.2 4.6 collective-permute-start.1
  750.8 23.8 %bitcast_add_fusion.3 = f32[1,1024,5120]{2,1,0:T(8,128)} fusion(f32[1024,5120,1]{1,0,2:T(8,128)} %fusion.39, f32[1,1024,5120]{2,1,0:T(8,128)} %get-tuple-element.85, pred[]{:T(512)S(6)} %compare.6, bf16[1,1,224,5120]{3,2,1,0:T(8,128)(2,1)} %collective-permute-done.2, bf16[1,1,224,5120]{3,2,1,0:T(8,128)(2,1)} %collective-permute-done, ...), kind=kOutput, calls=%fused_computation.clone.1 | convolution fusion | flops 4717477888 | bytes 74842120 | tf_op jit(solution)/gta,gtb->gab/dot_general | solution.py:19
  774.6 72.4 %collective-permute-done.1 = bf16[1,1,224,5120]{3,2,1,0:T(8,128)(2,1)S(1)} collective-permute-done((bf16[1,1,224,5120]{3,2,1,0:T(8,128)(2,1)}, bf16[1,1,224,5120]{3,2,1,0:T(8,128)(2,1)S(1)}, u32[]{:S(2)}, u32[]{:S(2)}) %collective-permute-start.1) | collective-permute-done | bytes 2293792 | tf_op jit(solution)/gta,gtb->gab/dot_general | solution.py:19
  847.0 4.6 collective-permute-start
  851.7 23.9 %collective-permute-start.2 = (bf16[1,1,224,5120]{3,2,1,0:T(8,128)(2,1)}, bf16[1,1,224,5120]{3,2,1,0:T(8,128)(2,1)}, u32[]{:S(2)}, u32[]{:S(2)}) collective-permute-start(bf16[1,1,224,5120]{3,2,1,0:T(8,128)(2,1)} %get-tuple-element.86), channel_id=11, source_target_pairs={{0,1},{1,2},{2,3},{3,4},{4,5},{5,6},{6,7},{7,8},{8,9},{9,10},{10,1... | collective-permute-start | bytes 6881288 | tf_op jit(solution)/gta,gtb->gab/dot_general | solution.py:19
  875.6 0.6 dynamic-slice.65
  878.1 11.5 %fusion.39 = f32[1024,5120,1]{1,0,2:T(8,128)} fusion(bf16[1,1,224,5120]{3,2,1,0:T(8,128)(2,1)} %get-tuple-element.86, bf16[1,1,224,5120]{3,2,1,0:T(8,128)(2,1)S(1)} %get-tuple-element.84, s32[]{:T(128)S(6)} %multiply.15, bf16[1,1,3584,1024]{3,2,1,0:T(8,128)(2,1)} %bitcast.65, s32[]{:T(128)S(6)} %multiply.16), kind=kOutput, calls=%fused_computation.7.clone.1 | convolution fusion | flops 4701749248 | bytes 32899080 | tf_op jit(solution)/gta,gtb->gab/dot_general | solution.py:19
  889.6 25.6 %collective-permute-done = bf16[1,1,224,5120]{3,2,1,0:T(8,128)(2,1)} collective-permute-done((bf16[1,1,224,5120]{3,2,1,0:T(8,128)(2,1)S(1)}, bf16[1,1,224,5120]{3,2,1,0:T(8,128)(2,1)}, u32[]{:S(2)}, u32[]{:S(2)}) %collective-permute-start) | collective-permute-done | bytes 2293792 | tf_op jit(solution)/gta,gtb->gab/dot_general | solution.py:19
  915.2 4.6 collective-permute-start.1
  919.8 18.2 %collective-permute-done.2 = bf16[1,1,224,5120]{3,2,1,0:T(8,128)(2,1)} collective-permute-done((bf16[1,1,224,5120]{3,2,1,0:T(8,128)(2,1)}, bf16[1,1,224,5120]{3,2,1,0:T(8,128)(2,1)}, u32[]{:S(2)}, u32[]{:S(2)}) %collective-permute-start.2) | collective-permute-done | bytes 2293792 | tf_op jit(solution)/gta,gtb->gab/dot_general | solution.py:19
  938.1 23.8 %bitcast_add_fusion.3 = f32[1,1024,5120]{2,1,0:T(8,128)} fusion(f32[1024,5120,1]{1,0,2:T(8,128)} %fusion.39, f32[1,1024,5120]{2,1,0:T(8,128)} %get-tuple-element.85, pred[]{:T(512)S(6)} %compare.6, bf16[1,1,224,5120]{3,2,1,0:T(8,128)(2,1)} %collective-permute-done.2, bf16[1,1,224,5120]{3,2,1,0:T(8,128)(2,1)} %collective-permute-done, ...), kind=kOutput, calls=%fused_computation.clone.1 | convolution fusion | flops 4717477888 | bytes 74842120 | tf_op jit(solution)/gta,gtb->gab/dot_general | solution.py:19
  961.9 5.1 collective-permute-done.1
  967.1 23.7 %collective-permute-done.3 = bf16[1,1,224,5120]{3,2,1,0:T(8,128)(2,1)} collective-permute-done((bf16[1,1,224,5120]{3,2,1,0:T(8,128)(2,1)}, bf16[1,1,224,5120]{3,2,1,0:T(8,128)(2,1)}, u32[]{:S(2)}, u32[]{:S(2)}) %collective-permute-start.3) | collective-permute-done | bytes 2293792 | tf_op jit(solution)/gta,gtb->gab/dot_general | solution.py:19
  990.8 0.5 collective-permute-start.2
  991.3 0.6 dynamic-slice.65
  993.8 11.5 %fusion.39 = f32[1024,5120,1]{1,0,2:T(8,128)} fusion(bf16[1,1,224,5120]{3,2,1,0:T(8,128)(2,1)} %get-tuple-element.86, bf16[1,1,224,5120]{3,2,1,0:T(8,128)(2,1)S(1)} %get-tuple-element.84, s32[]{:T(128)S(6)} %multiply.15, bf16[1,1,3584,1024]{3,2,1,0:T(8,128)(2,1)} %bitcast.65, s32[]{:T(128)S(6)} %multiply.16), kind=kOutput, calls=%fused_computation.7.clone.1 | convolution fusion | flops 4701749248 | bytes 32899080 | tf_op jit(solution)/gta,gtb->gab/dot_general | solution.py:19
  1005.3 35.5 %collective-permute-done = bf16[1,1,224,5120]{3,2,1,0:T(8,128)(2,1)} collective-permute-done((bf16[1,1,224,5120]{3,2,1,0:T(8,128)(2,1)S(1)}, bf16[1,1,224,5120]{3,2,1,0:T(8,128)(2,1)}, u32[]{:S(2)}, u32[]{:S(2)}) %collective-permute-start) | collective-permute-done | bytes 2293792 | tf_op jit(solution)/gta,gtb->gab/dot_general | solution.py:19
  1040.8 4.6 collective-permute-start.1
  1045.5 23.8 %bitcast_add_fusion.3 = f32[1,1024,5120]{2,1,0:T(8,128)} fusion(f32[1024,5120,1]{1,0,2:T(8,128)} %fusion.39, f32[1,1024,5120]{2,1,0:T(8,128)} %get-tuple-element.85, pred[]{:T(512)S(6)} %compare.6, bf16[1,1,224,5120]{3,2,1,0:T(8,128)(2,1)} %collective-permute-done.2, bf16[1,1,224,5120]{3,2,1,0:T(8,128)(2,1)} %collective-permute-done, ...), kind=kOutput, calls=%fused_computation.clone.1 | convolution fusion | flops 4717477888 | bytes 74842120 | tf_op jit(solution)/gta,gtb->gab/dot_general | solution.py:19
  1069.3 23.5 %collective-permute-done.1 = bf16[1,1,224,5120]{3,2,1,0:T(8,128)(2,1)S(1)} collective-permute-done((bf16[1,1,224,5120]{3,2,1,0:T(8,128)(2,1)}, bf16[1,1,224,5120]{3,2,1,0:T(8,128)(2,1)S(1)}, u32[]{:S(2)}, u32[]{:S(2)}) %collective-permute-start.1) | collective-permute-done | bytes 2293792 | tf_op jit(solution)/gta,gtb->gab/dot_general | solution.py:19
  1092.8 12.3 %convert_bitcast_fusion.2 = bf16[1024,5120]{1,0:T(8,128)(2,1)} fusion(f32[1,1024,5120]{2,1,0:T(8,128)} %get-tuple-element.6), kind=kLoop, calls=%fused_computation.38 | loop fusion | flops 5242880 | bytes 31457280 | tf_op jit(solution)/reshape | solution.py:20
  (23 shorter events, 0.2 us)
Async XLA Ops:
  7.2 188.9 %all-gather.9.cloned.1.call-start = ((), (), s32[]{:S(2)}) async-start(), calls=%async_computation.1 | async-start | bytes 38993920 | tf_op args[1]
  10.4 377.6 %all-gather.11.cloned.1.call-start = ((), (), s32[]{:S(2)}) async-start(), calls=%async_computation.2 | async-start | bytes 38993920 | tf_op jit(solution)/reshape | solution.py:18
  11.2 1093.9 %reduce-scatter.4.cloned.1.call-start = ((), (), s32[]{:S(2)}) async-start(), calls=%async_computation.3 | async-start | bytes 38993920
  386.2 1.6 copy-start
  387.8 132.2 %collective-permute-start.4 = (bf16[1,1,224,5120]{3,2,1,0:T(8,128)(2,1)S(1)}, bf16[1,1,224,5120]{3,2,1,0:T(8,128)(2,1)}, u32[]{:S(2)}, u32[]{:S(2)}) collective-permute-start(bf16[1,1,224,5120]{3,2,1,0:T(8,128)(2,1)S(1)} %bitcast.67), channel_id=9, source_target_pairs={{0,1},{1,2},{2,3},{3,4},{4,5},{5,6},{6,7},{7,8},{8,9},{9,10},{10,1... | collective-permute-start | bytes 6881288 | tf_op jit(solution)/gta,gtb->gab/dot_general | solution.py:19
  505.6 14.4 %copy-start.1 = (u32[32]{0:T(128)S(1)}, u32[32]{0:T(128)}, u32[]{:S(2)}) copy-start(u32[32]{0:T(128)} %constant.146) | copy-start | bytes 388
  520.2 103.0 %collective-permute-start = (bf16[1,1,224,5120]{3,2,1,0:T(8,128)(2,1)S(1)}, bf16[1,1,224,5120]{3,2,1,0:T(8,128)(2,1)}, u32[]{:S(2)}, u32[]{:S(2)}) collective-permute-start(bf16[1,1,224,5120]{3,2,1,0:T(8,128)(2,1)S(1)} %get-tuple-element.84), channel_id=10, source_target_pairs={{0,15},{1,0},{2,1},{3,2},{4,3},{5,4},{6,5},{7,6},{8,7},{9,8},{10,9... | collective-permute-start | bytes 6881288 | tf_op jit(solution)/gta,gtb->gab/dot_general | solution.py:19
  524.4 103.4 %collective-permute-start.2 = (bf16[1,1,224,5120]{3,2,1,0:T(8,128)(2,1)}, bf16[1,1,224,5120]{3,2,1,0:T(8,128)(2,1)}, u32[]{:S(2)}, u32[]{:S(2)}) collective-permute-start(bf16[1,1,224,5120]{3,2,1,0:T(8,128)(2,1)} %get-tuple-element.86), channel_id=11, source_target_pairs={{0,1},{1,2},{2,3},{3,4},{4,5},{5,6},{6,7},{7,8},{8,9},{9,10},{10,1... | collective-permute-start | bytes 6881288 | tf_op jit(solution)/gta,gtb->gab/dot_general | solution.py:19
  623.2 60.6 %collective-permute-start.1 = (bf16[1,1,224,5120]{3,2,1,0:T(8,128)(2,1)}, bf16[1,1,224,5120]{3,2,1,0:T(8,128)(2,1)S(1)}, u32[]{:S(2)}, u32[]{:S(2)}) collective-permute-start(bf16[1,1,224,5120]{3,2,1,0:T(8,128)(2,1)} %collective-permute-done), channel_id=12, source_target_pairs={{0,15},{1,0},{2,1},{3,2},{4,3},{5,4},{6,5},{7,6},{8,7},{9,8},{10,9... | collective-permute-start | bytes 6881288 | tf_op jit(solution)/gta,gtb->gab/dot_general | solution.py:19
  627.9 69.0 %collective-permute-start.3 = (bf16[1,1,224,5120]{3,2,1,0:T(8,128)(2,1)}, bf16[1,1,224,5120]{3,2,1,0:T(8,128)(2,1)}, u32[]{:S(2)}, u32[]{:S(2)}) collective-permute-start(bf16[1,1,224,5120]{3,2,1,0:T(8,128)(2,1)} %collective-permute-done.2), channel_id=13, source_target_pairs={{0,1},{1,2},{2,3},{3,4},{4,5},{5,6},{6,7},{7,8},{8,9},{9,10},{10,1... | collective-permute-start | bytes 6881288 | tf_op jit(solution)/gta,gtb->gab/dot_general | solution.py:19
  696.8 49.3 %collective-permute-start = (bf16[1,1,224,5120]{3,2,1,0:T(8,128)(2,1)S(1)}, bf16[1,1,224,5120]{3,2,1,0:T(8,128)(2,1)}, u32[]{:S(2)}, u32[]{:S(2)}) collective-permute-start(bf16[1,1,224,5120]{3,2,1,0:T(8,128)(2,1)S(1)} %get-tuple-element.84), channel_id=10, source_target_pairs={{0,15},{1,0},{2,1},{3,2},{4,3},{5,4},{6,5},{7,6},{8,7},{9,8},{10,9... | collective-permute-start | bytes 6881288 | tf_op jit(solution)/gta,gtb->gab/dot_general | solution.py:19
  696.8 54.0 %collective-permute-start.2 = (bf16[1,1,224,5120]{3,2,1,0:T(8,128)(2,1)}, bf16[1,1,224,5120]{3,2,1,0:T(8,128)(2,1)}, u32[]{:S(2)}, u32[]{:S(2)}) collective-permute-start(bf16[1,1,224,5120]{3,2,1,0:T(8,128)(2,1)} %get-tuple-element.86), channel_id=11, source_target_pairs={{0,1},{1,2},{2,3},{3,4},{4,5},{5,6},{6,7},{7,8},{8,9},{9,10},{10,1... | collective-permute-start | bytes 6881288 | tf_op jit(solution)/gta,gtb->gab/dot_general | solution.py:19
  746.2 100.9 %collective-permute-start.1 = (bf16[1,1,224,5120]{3,2,1,0:T(8,128)(2,1)}, bf16[1,1,224,5120]{3,2,1,0:T(8,128)(2,1)S(1)}, u32[]{:S(2)}, u32[]{:S(2)}) collective-permute-start(bf16[1,1,224,5120]{3,2,1,0:T(8,128)(2,1)} %collective-permute-done), channel_id=12, source_target_pairs={{0,15},{1,0},{2,1},{3,2},{4,3},{5,4},{6,5},{7,6},{8,7},{9,8},{10,9... | collective-permute-start | bytes 6881288 | tf_op jit(solution)/gta,gtb->gab/dot_general | solution.py:19
  750.8 96.3 %collective-permute-start.3 = (bf16[1,1,224,5120]{3,2,1,0:T(8,128)(2,1)}, bf16[1,1,224,5120]{3,2,1,0:T(8,128)(2,1)}, u32[]{:S(2)}, u32[]{:S(2)}) collective-permute-start(bf16[1,1,224,5120]{3,2,1,0:T(8,128)(2,1)} %collective-permute-done.2), channel_id=13, source_target_pairs={{0,1},{1,2},{2,3},{3,4},{4,5},{5,6},{6,7},{7,8},{8,9},{9,10},{10,1... | collective-permute-start | bytes 6881288 | tf_op jit(solution)/gta,gtb->gab/dot_general | solution.py:19
  847.0 68.1 %collective-permute-start = (bf16[1,1,224,5120]{3,2,1,0:T(8,128)(2,1)S(1)}, bf16[1,1,224,5120]{3,2,1,0:T(8,128)(2,1)}, u32[]{:S(2)}, u32[]{:S(2)}) collective-permute-start(bf16[1,1,224,5120]{3,2,1,0:T(8,128)(2,1)S(1)} %get-tuple-element.84), channel_id=10, source_target_pairs={{0,15},{1,0},{2,1},{3,2},{4,3},{5,4},{6,5},{7,6},{8,7},{9,8},{10,9... | collective-permute-start | bytes 6881288 | tf_op jit(solution)/gta,gtb->gab/dot_general | solution.py:19
  851.7 86.4 %collective-permute-start.2 = (bf16[1,1,224,5120]{3,2,1,0:T(8,128)(2,1)}, bf16[1,1,224,5120]{3,2,1,0:T(8,128)(2,1)}, u32[]{:S(2)}, u32[]{:S(2)}) collective-permute-start(bf16[1,1,224,5120]{3,2,1,0:T(8,128)(2,1)} %get-tuple-element.86), channel_id=11, source_target_pairs={{0,1},{1,2},{2,3},{3,4},{4,5},{5,6},{6,7},{7,8},{8,9},{9,10},{10,1... | collective-permute-start | bytes 6881288 | tf_op jit(solution)/gta,gtb->gab/dot_general | solution.py:19
  915.2 51.9 %collective-permute-start.1 = (bf16[1,1,224,5120]{3,2,1,0:T(8,128)(2,1)}, bf16[1,1,224,5120]{3,2,1,0:T(8,128)(2,1)S(1)}, u32[]{:S(2)}, u32[]{:S(2)}) collective-permute-start(bf16[1,1,224,5120]{3,2,1,0:T(8,128)(2,1)} %collective-permute-done), channel_id=12, source_target_pairs={{0,15},{1,0},{2,1},{3,2},{4,3},{5,4},{6,5},{7,6},{8,7},{9,8},{10,9... | collective-permute-start | bytes 6881288 | tf_op jit(solution)/gta,gtb->gab/dot_general | solution.py:19
  938.1 52.7 %collective-permute-start.3 = (bf16[1,1,224,5120]{3,2,1,0:T(8,128)(2,1)}, bf16[1,1,224,5120]{3,2,1,0:T(8,128)(2,1)}, u32[]{:S(2)}, u32[]{:S(2)}) collective-permute-start(bf16[1,1,224,5120]{3,2,1,0:T(8,128)(2,1)} %collective-permute-done.2), channel_id=13, source_target_pairs={{0,1},{1,2},{2,3},{3,4},{4,5},{5,6},{6,7},{7,8},{8,9},{9,10},{10,1... | collective-permute-start | bytes 6881288 | tf_op jit(solution)/gta,gtb->gab/dot_general | solution.py:19
  990.8 50.0 %collective-permute-start = (bf16[1,1,224,5120]{3,2,1,0:T(8,128)(2,1)S(1)}, bf16[1,1,224,5120]{3,2,1,0:T(8,128)(2,1)}, u32[]{:S(2)}, u32[]{:S(2)}) collective-permute-start(bf16[1,1,224,5120]{3,2,1,0:T(8,128)(2,1)S(1)} %get-tuple-element.84), channel_id=10, source_target_pairs={{0,15},{1,0},{2,1},{3,2},{4,3},{5,4},{6,5},{7,6},{8,7},{9,8},{10,9... | collective-permute-start | bytes 6881288 | tf_op jit(solution)/gta,gtb->gab/dot_general | solution.py:19
  990.8 54.7 %collective-permute-start.2 = (bf16[1,1,224,5120]{3,2,1,0:T(8,128)(2,1)}, bf16[1,1,224,5120]{3,2,1,0:T(8,128)(2,1)}, u32[]{:S(2)}, u32[]{:S(2)}) collective-permute-start(bf16[1,1,224,5120]{3,2,1,0:T(8,128)(2,1)} %get-tuple-element.86), channel_id=11, source_target_pairs={{0,1},{1,2},{2,3},{3,4},{4,5},{5,6},{6,7},{7,8},{8,9},{9,10},{10,1... | collective-permute-start | bytes 6881288 | tf_op jit(solution)/gta,gtb->gab/dot_general | solution.py:19
  1040.8 52.0 %collective-permute-start.1 = (bf16[1,1,224,5120]{3,2,1,0:T(8,128)(2,1)}, bf16[1,1,224,5120]{3,2,1,0:T(8,128)(2,1)S(1)}, u32[]{:S(2)}, u32[]{:S(2)}) collective-permute-start(bf16[1,1,224,5120]{3,2,1,0:T(8,128)(2,1)} %collective-permute-done), channel_id=12, source_target_pairs={{0,15},{1,0},{2,1},{3,2},{4,3},{5,4},{6,5},{7,6},{8,7},{9,8},{10,9... | collective-permute-start | bytes 6881288 | tf_op jit(solution)/gta,gtb->gab/dot_general | solution.py:19
  1045.5 47.3 %collective-permute-start.3 = (bf16[1,1,224,5120]{3,2,1,0:T(8,128)(2,1)}, bf16[1,1,224,5120]{3,2,1,0:T(8,128)(2,1)}, u32[]{:S(2)}, u32[]{:S(2)}) collective-permute-start(bf16[1,1,224,5120]{3,2,1,0:T(8,128)(2,1)} %collective-permute-done.2), channel_id=13, source_target_pairs={{0,1},{1,2},{2,3},{3,4},{4,5},{5,6},{6,7},{7,8},{8,9},{9,10},{10,1... | collective-permute-start | bytes 6881288 | tf_op jit(solution)/gta,gtb->gab/dot_general | solution.py:19
Sparse Core Ops, SparseCore 0:
  10.5 185.4 all-gather.8
  197.7 182.7 all-gather.10
  386.3 502.8 reduce-scatter.3
where the time goes:
time: 1120 us; the launch traced here: 1110 us
  waiting for transfers between devices  538 us (48%)
  matrix products  413 us (37%)
  starting transfers between devices  73.5 us (7%)
  local copies, waits for them, and re-layouts  35.9 us (3%)
  other arithmetic  29.3 us (3%)
  between operations  13.9 us (1%)
    dot_general x17, waiting for transfers between devices, by_group(): jnp.einsum('gta,gtb->gab', a, b, preferred_element_type=jnp.float32)  352 us
    dot_general x10, matrix products, by_group(): jnp.einsum('gta,gtb->gab', a, b, preferred_element_type=jnp.float32)  240 us
    unnamed x5, waiting for transfers between devices  186 us
    dot_general x2, matrix products, step(): dx = jnp.dot(d_gate, w_gate.T) + jnp.dot(d_up, w_up.T)  126 us
    dot_general x17, starting transfers between devices, by_group(): jnp.einsum('gta,gtb->gab', a, b, preferred_element_type=jnp.float32)  73.4 us
    dot_general x1, matrix products, step(): d_hidden = jnp.dot(dy, w_down.T, preferred_element_type=jnp.float32)  47.1 us
    unnamed x7, local copies, waits for them, and re-layouts  33.6 us
  transfers between devices with their start and end apart: 20, of which 12 were waited for; matrix products, arithmetic and copies ran while one was open for 43% of the time, Pallas kernels for 0%

commit v1 on v0

v1 whole, which is shorter than its diff:
```python
import functools

import jax
import jax.numpy as jnp
from jax import lax
from jax.experimental import pallas as pl
from jax.experimental.pallas import tpu as pltpu
from jax.sharding import PartitionSpec as P

MESH = pl.DeviceIdType.MESH
BF16, F32 = jnp.bfloat16, jnp.float32
NC = 4
BLOCKS = 8
LAG = 2
KEEP = 3
Y_X, RS_Y = 16, 32
A_END, B_END, N_END, L_T, C_END = 20, 25, 29, 33, 36


def order(p, z):
    near = jnp.where(z < 2, z, 3 - z)
    q = jnp.where((near == 1) & (p < 2), 1 - p, p)
    return jnp.where(z < 2, q, 3 - q)


def kernel(
    dims,
    x, dy, gate, up, wg, wu, wd,
    dx, dwg, dwu, dwd, gx, gdy, own, sib, ins, yin, dgs, dus, hids,
    own_b, sib_b, in_b, out_b,
    z_send, z_recv, y_send, y_recv, sib_send, sib_recv, own_send,
    rs_send, rs_recv, ry_send, ry_recv, dxs_recv, load_sem,
):
    R, D, F, TF, TN, TM, TM2, TND, TK, TV = dims
    C, B, T = R // NC, 2 * R, 2 * R * BLOCKS
    dp, tp = lax.axis_index("dp"), lax.axis_index("tp")
    y, z, c = tp // 8, (tp // 2) % 4, tp % 2
    sent, kept = (dy, x), (gdy, gx)

    def dev(yy, zz, cc):
        return dict(device_id=(dp, yy * 8 + zz * 2 + cc), device_id_type=MESH)

    def rows(ref, start, n):
        return ref.at[pl.ds(pl.multiple_of(start, 8), n)]

    def place(yy, zz, cc):
        return ((yy * 4 + zz) * 2 + cc) * R

    def step_of(d):
        return (z, jnp.minimum(z + 1, 3)) if d == 0 else (3 - z, jnp.maximum(z - 1, 0))

    def z_at(d, pos):
        return pos if d == 0 else 3 - pos

    def gather_z(d, a, t):
        pos, nxt = step_of(d)
        base = a * NC * (pos + 1)

        def copy(t, own_rows=False):
            s = jnp.clip(t - base, 0, 11)
            p, j = s // NC, s % NC
            there = rows(kept[a], place(y, z_at(d, jnp.maximum(pos - p, 0)), c) + j * C, C)
            src = rows(sent[a], j * C, C) if own_rows else there
            return pltpu.make_async_remote_copy(
                src, there, z_send.at[d, a, t % 4], z_recv.at[d, a, s], **dev(y, nxt, c))

        def active(t):
            return (pos < 3) & (t >= base) & (t < base + NC * (pos + 1))

        @pl.when(active(t - KEEP))
        def _():
            copy(t - KEEP).wait_send()

        @pl.when(active(t) & (t < base + NC))
        def _():
            copy(t, True).start()

        @pl.when(active(t) & (t >= base + NC))
        def _():
            copy(t).start()

    def to_sibling(a, ref_rows, idx, sem):
        return pltpu.make_async_remote_copy(ref_rows, ref_rows, sem, sib_recv.at[a, idx], **dev(y, z, 1 - c))

    def arrive_z(d, a, t):
        pos, _ = step_of(d)
        base = a * NC * pos + LAG

        def chunk(t):
            r = jnp.clip(t - base, 0, 11)
            src_z = z_at(d, jnp.maximum(pos - 1 - r // NC, 0))
            return r, rows(kept[a], place(y, src_z, c) + (r % NC) * C, C), y * 4 + src_z

        def active(t):
            return (pos > 0) & (t >= base) & (t < base + NC * pos)

        @pl.when(active(t - KEEP))
        def _():
            _, ref, idx = chunk(t - KEEP)
            to_sibling(a, ref, idx, sib_send.at[d, a, (t - KEEP) % 4]).wait_send()

        @pl.when(active(t))
        def _():
            r, ref, idx = chunk(t)
            pltpu.make_async_remote_copy(
                ref, ref, z_send.at[d, a, 0], z_recv.at[d, a, r], **dev(y, z, 1 - c)).wait_recv()
            to_sibling(a, ref, idx, sib_send.at[d, a, t % 4]).start()

    def gather_y(a, t):
        base = a * Y_X

        def copy(t, own_rows=False):
            s = jnp.clip(t - base, 0, 15)
            there = rows(kept[a], place(y, order(s // NC, z), c) + (s % NC) * C, C)
            src = rows(sent[a], (s % NC) * C, C) if own_rows else there
            return pltpu.make_async_remote_copy(
                src, there, y_send.at[a, t % 4], y_recv.at[a, s], **dev(1 - y, z, c))

        def active(t):
            return (t >= base) & (t < base + 4 * NC)

        @pl.when(active(t - KEEP))
        def _():
            copy(t - KEEP).wait_send()

        @pl.when(active(t) & (t < base + NC))
        def _():
            copy(t, True).start()

        @pl.when(active(t) & (t >= base + NC))
        def _():
            copy(t).start()

    def arrive_y(a, t, drain_only=False):
        base = a * Y_X + LAG

        def chunk(t):
            r = jnp.clip(t - base, 0, 15)
            q = order(r // NC, z)
            return r, rows(kept[a], place(1 - y, q, c) + (r % NC) * C, C), (1 - y) * 4 + q

        def active(t):
            return (t >= base) & (t < base + 4 * NC)

        @pl.when(active(t - KEEP))
        def _():
            _, ref, idx = chunk(t - KEEP)
            to_sibling(a, ref, idx, sib_send.at[2, a, (t - KEEP) % 4]).wait_send()

        if drain_only:
            return

        @pl.when(active(t))
        def _():
            r, ref, idx = chunk(t)
            pltpu.make_async_remote_copy(
                ref, ref, y_send.at[a, 0], y_recv.at[a, r], **dev(1 - y, z, c)).wait_recv()
            to_sibling(a, ref, idx, sib_send.at[2, a, t % 4]).start()

    def own_to_sibling(a):
        return pltpu.make_async_remote_copy(
            sent[a], rows(kept[a], place(y, z, c), R), own_send.at[a], sib_recv.at[a, y * 4 + z], **dev(y, z, 1 - c))

    def wait_sibling(a, idx):
        ref = rows(kept[a], idx * B, R)
        pltpu.make_async_remote_copy(ref, ref, own_send.at[a], sib_recv.at[a, idx], **dev(y, z, 1 - c)).wait_recv()

    def wait_partial(idx):
        ref = rows(sib, idx * R, R)
        pltpu.make_async_remote_copy(ref, ref, own_send.at[0], dxs_recv.at[idx], **dev(y, z, 1 - c)).wait_recv()

    def own_load(b, idx, j):
        return pltpu.make_async_copy(rows(own, idx * R + j * C, C), own_b.at[b], load_sem.at[b, 0])

    def sib_load(b, idx, j):
        return pltpu.make_async_copy(rows(sib, idx * R + j * C, C), sib_b.at[b], load_sem.at[b, 1])

    def in_load(b, n, d, k, j):
        return pltpu.make_async_copy(rows(ins.at[d], k * R + j * C, C), in_b.at[b, n], load_sem.at[b, 2 + n])

    def wait_in(d, k, j):
        ref = rows(ins.at[d], k * R + j * C, C)
        pltpu.make_async_remote_copy(
            ref, ref, rs_send.at[d, 0], rs_recv.at[d, k * NC + j], **dev(y, z, 1 - c)).wait_recv()

    def add(b, slot, n):
        @pl.loop(0, D // TV)
        def _(i):
            cols = pl.ds(pl.multiple_of(i * TV, 128), TV)
            total = own_b[b, :, cols] + sib_b[b, :, cols].astype(F32)
            for m in range(n):
                total = total + in_b[b, m, :, cols].astype(F32)
            out_b[b, slot, :, cols] = total.astype(BF16)

    def sum_state(d, t):
        pos, nxt = step_of(d)
        base = jnp.where(pos == 0, 9, jnp.where(pos == 1, 11, 16))
        first = jnp.where(pos == 0, 0, 2)
        last = jnp.where(pos == 2, 4, 6)
        on = (pos < 3) & (t >= base + NC * first) & (t < base + NC * last)
        u = jnp.clip(t - base, 0, 23)
        k, j = u // NC, u % NC
        to_pos = jnp.where(k < 2, 1, jnp.where(k < 4, 3, 2))
        other = (k == 1) | (k == 3) | (k == 4)
        idx = jnp.where(other, 1 - y, y) * 4 + z_at(d, to_pos)
        return on, pos, nxt, k, j, idx

    def sum_send(d, t, nxt, k, j):
        return pltpu.make_async_remote_copy(
            out_b.at[d, t % 3], rows(ins.at[d], k * R + j * C, C), rs_send.at[d, t % 3],
            rs_recv.at[d, k * NC + j], **dev(y, nxt, c))

    def sum_loads(d, t):
        on, pos, _, k, j, idx = sum_state(d, t)

        @pl.when(on)
        def _():
            @pl.when(j == 0)
            def _():
                wait_partial(idx)

            own_load(d, idx, j).start()
            sib_load(d, idx, j).start()

            @pl.when(pos > 0)
            def _():
                wait_in(d, k, j)
                in_load(d, 0, d, k, j).start()

    def sum_drain(d, t):
        was, _, nxt, k, j, _ = sum_state(d, t - KEEP)

        @pl.when(was)
        def _():
            sum_send(d, t - KEEP, nxt, k, j).wait_send()

    def sum_add(d, t):
        sum_drain(d, t)
        on, pos, nxt, k, j, idx = sum_state(d, t)

        @pl.when(on)
        def _():
            own_load(d, idx, j).wait()
            sib_load(d, idx, j).wait()

            @pl.when(pos > 0)
            def _():
                in_load(d, 0, d, k, j).wait()
                add(d, t % 3, 1)

            @pl.when(pos == 0)
            def _():
                add(d, t % 3, 0)

            sum_send(d, t, nxt, k, j).start()

    def last_in(pos, other):
        if other:
            return jnp.where(pos == 1, 1, jnp.where(pos == 2, 4, 3))
        return jnp.where(pos == 1, 0, jnp.where(pos == 2, 5, 2))

    def end_loads(b, j, other, start):
        idx = jnp.where(other, 1 - y, y) * 4 + z
        if start:
            @pl.when(j == 0)
            def _():
                wait_partial(idx)

        copies = [own_load(b, idx, j), sib_load(b, idx, j)]
        for copy in copies:
            copy.start() if start else copy.wait()
        for d, there, slot in ((0, z > 0, 0), (1, z < 3, jnp.where(z > 0, 1, 0))):
            pos, _ = step_of(d)
            k = last_in(pos, other)

            @pl.when(there)
            def _(d=d, k=k, slot=slot):
                if start:
                    wait_in(d, k, j)
                    in_load(b, slot, d, k, j).start()
                else:
                    in_load(b, slot, d, k, j).wait()

    middle = (z > 0) & (z < 3)
    y_set = jnp.where(z < 2, 1, 0)

    def y_copy(t):
        j = jnp.clip(t - RS_Y, 0, NC - 1)
        return pltpu.make_async_remote_copy(
            out_b.at[y_set, t % 3], rows(yin, j * C, C), ry_send.at[t % 3], ry_recv.at[j], **dev(1 - y, z, c))

    def y_on(t):
        return (t >= RS_Y) & (t < RS_Y + NC)

    def y_drain(t):
        @pl.when(y_on(t - KEEP))
        def _():
            y_copy(t - KEEP).wait_send()

    def y_loads(t):
        @pl.when(y_on(t))
        def _():
            end_loads(y_set, t - RS_Y, True, True)

    def y_sum(t):
        y_drain(t)

        @pl.when(y_on(t))
        def _():
            end_loads(y_set, t - RS_Y, True, False)

            @pl.when(middle)
            def _():
                add(y_set, t % 3, 2)

            @pl.when(jnp.logical_not(middle))
            def _():
                add(y_set, t % 3, 1)

            y_copy(t).start()

    def clear(ref):
        high = min(64, ref.shape[0])

        @pl.loop(0, ref.shape[0] // high)
        def _(i):
            ref[pl.ds(pl.multiple_of(i * high, 8), high), :] = jnp.zeros((high, ref.shape[1]), F32)

    def exchange(t, late):
        for a in (0, 1):
            for d in (0, 1):
                arrive_z(d, a, t)
            arrive_y(a, t)
        for a in (0, 1):
            gather_y(a, t)
            for d in (0, 1):
                gather_z(d, a, t)
        for d in (0, 1):
            sum_loads(d, t)
        if late:
            y_loads(t)

    def sums(t, late):
        for d in (0, 1):
            sum_add(d, t)
        if late:
            y_sum(t)

    def spread(t, late, begin, end, step):
        @pl.loop(0, jnp.maximum(end - begin, 2))
        def _(n):
            @pl.when(n == 1)
            def _():
                sums(t, late)

            @pl.when(begin + n < end)
            def _():
                step(begin + n)

    barrier = pltpu.get_barrier_semaphore()
    pl.semaphore_signal(barrier, 1, **dev(y, z, 1 - c))
    pl.semaphore_signal(barrier, 1, **dev(1 - y, z, c))

    @pl.when(z < 3)
    def _():
        pl.semaphore_signal(barrier, 1, **dev(y, z + 1, c))

    @pl.when(z > 0)
    def _():
        pl.semaphore_signal(barrier, 1, **dev(y, z - 1, c))

    pl.semaphore_wait(barrier, jnp.where((z > 0) & (z < 3), 4, 3))
    for a in (0, 1):
        own_to_sibling(a).start()

    def first(wd_v, wg_v, wu_v, dy_v, gate_v, up_v, dg_v, du_v, hid_v, stf, stb, w_sem, b_sem, dy_sem, g_sem, st_sem, dx_sem, dxs_send):
        weights = [pltpu.make_async_copy(h, v, w_sem.at[i]) for i, (h, v) in enumerate(((wd, wd_v), (wg, wg_v), (wu, wu_v)))]

        def block_of(n):
            other = (n // 2) % 2
            return jnp.where(other == 1, 1 - y, y) * 4 + order(n % 2 + 2 * (n // 4), z)

        def gate_up(n):
            at = block_of(n) * B
            return [pltpu.make_async_copy(rows(h, at, B), v, g_sem.at[i]) for i, (h, v) in enumerate(((gate, gate_v), (up, up_v)))]

        def kept_grads(n):
            at = block_of(n) * B
            pairs = ((dg_v, dgs), (du_v, dus), (hid_v, hids))
            return [pltpu.make_async_copy(v, rows(h, at, B), st_sem.at[i]) for i, (v, h) in enumerate(pairs)]

        def own_rows(i, a):
            part = rows(dy_v, a * R, R)
            if i == 0:
                return pltpu.make_async_copy(sent[a], part, b_sem.at[a])
            return pltpu.make_async_copy(part, rows(kept[a], place(y, z, c), R), b_sem.at[a])

        def terms(n, tile, slot):
            at, cols = block_of(n) * R, pl.ds(pl.multiple_of(tile * TN, 128), TN)
            mine = pltpu.make_async_copy(
                stf.at[slot, pl.ds(pl.multiple_of(c * R, 8), R)], own.at[pl.ds(pl.multiple_of(at, 8), R), cols], dx_sem.at[slot])
            theirs = pltpu.make_async_remote_copy(
                stb.at[slot, pl.ds(pl.multiple_of((1 - c) * R, 8), R)], sib.at[pl.ds(pl.multiple_of(at, 8), R), cols],
                dxs_send.at[slot], dxs_recv.at[block_of(n)], **dev(y, z, 1 - c))
            return mine, theirs

        def wait_terms(n, tile, slot):
            mine, theirs = terms(n, tile, slot)
            mine.wait()
            theirs.wait_send()

        tiles = D // TN

        def drain(n):
            for copy in kept_grads(n):
                copy.wait()
            for slot in (0, 1):
                wait_terms(n, tiles - 2 + slot, slot)

        def gradients(n):
            @pl.when(n == 0)
            def _():
                weights[0].wait()

            for copy in gate_up(n):
                copy.wait()

            @pl.loop(0, F // TF)
            def _(i):
                cols = pl.ds(pl.multiple_of(i * TF, 128), TF)
                dh = lax.dot_general(
                    dy_v[...], wd_v[pl.ds(pl.multiple_of(i * TF, 128), TF), :], (((1,), (1,)), ((), ())), preferred_element_type=F32)
                g, u = gate_v[:, cols].astype(F32), up_v[:, cols].astype(F32)
                s = jax.nn.sigmoid(g)
                silu = g * s
                hid_v[:, cols] = (silu * u).astype(BF16)
                du_v[:, cols] = (dh * silu).astype(BF16)
                dg_v[:, cols] = ((dh * u) * (s * (1.0 + g * (1.0 - s)))).astype(BF16)

            for copy in kept_grads(n):
                copy.start()

            @pl.when(n < BLOCKS - 1)
            def _():
                for copy in gate_up(n + 1):
                    copy.start()

        def dx_terms(t, n):
            @pl.when(n == 0)
            def _():
                weights[1].wait()
                weights[2].wait()

            @pl.loop(0, tiles)
            def _(tile):
                @pl.when(tile == 1)
                def _():
                    sums(t, False)

                slot = tile % 2
                @pl.when(tile >= 2)
                def _():
                    wait_terms(n, tile - 2, slot)

                at = pl.ds(pl.multiple_of(tile * TN, 128), TN)
                nt = (((1,), (1,)), ((), ()))
                total = lax.dot_general(dg_v[...], wg_v[at, :], nt, preferred_element_type=F32)
                total = total + lax.dot_general(du_v[...], wu_v[at, :], nt, preferred_element_type=F32)
                stf[slot] = total
                stb[slot] = total.astype(BF16)
                mine, theirs = terms(n, tile, slot)
                mine.start()
                theirs.start()

        @pl.loop(0, A_END)
        def _(t):
            exchange(t, False)

            @pl.when(t == 0)
            def _():
                for a in (0, 1):
                    own_rows(0, a).start()
                for copy in gate_up(0) + weights:
                    copy.start()

            @pl.when(t == 1)
            def _():
                for a in (0, 1):
                    own_rows(0, a).wait()
                    own_rows(1, a).start()
                for a in (0, 1):
                    own_rows(1, a).wait()

            n = jnp.maximum((t - 4) // 2, 0)

            @pl.when((t == 2) | ((t >= 6) & (t % 2 == 0)))
            def _():
                idx = block_of(n)
                wait_sibling(0, idx)
                load = pltpu.make_async_copy(rows(gdy, idx * B, B), dy_v, dy_sem)
                load.start()

                @pl.when(n > 0)
                def _():
                    drain(n - 1)

                sums(t, False)
                load.wait()
                gradients(n)

            @pl.when((t == 3) | ((t >= 7) & (t % 2 == 1)))
            def _():
                dx_terms(t, n)

        drain(BLOCKS - 1)

    pl.run_scoped(
        first,
        pltpu.VMEM((F, D), BF16), pltpu.VMEM((D, F), BF16), pltpu.VMEM((D, F), BF16),
        pltpu.VMEM((B, D), BF16), pltpu.VMEM((B, F), BF16), pltpu.VMEM((B, F), BF16),
        pltpu.VMEM((B, F), BF16), pltpu.VMEM((B, F), BF16), pltpu.VMEM((B, F), BF16),
        pltpu.VMEM((2, B, TN), F32), pltpu.VMEM((2, B, TN), BF16),
        pltpu.SemaphoreType.DMA((3,)), pltpu.SemaphoreType.DMA((2,)), pltpu.SemaphoreType.DMA,
        pltpu.SemaphoreType.DMA((2,)), pltpu.SemaphoreType.DMA((3,)), pltpu.SemaphoreType.DMA((2,)), pltpu.SemaphoreType.DMA((2,)),
    )

    def second(hid_v, dy_v, acc, out_v, h_sem, dy_sem, o_sem):
        depth, wide = T // TK, D // TND
        steps = depth * wide
        per_tick = -(-steps // (B_END - A_END))

        def tile(i):
            nt, kc = i // depth, i % depth
            return pltpu.make_async_copy(
                gdy.at[pl.ds(pl.multiple_of(kc * TK, 8), TK), pl.ds(pl.multiple_of(nt * TND, 128), TND)],
                dy_v.at[i % 2], dy_sem.at[i % 2])

        def result(nt):
            return pltpu.make_async_copy(out_v, dwd.at[:, pl.ds(pl.multiple_of(nt * TND, 128), TND)], o_sem)

        hidden = pltpu.make_async_copy(hids, hid_v, h_sem)
        hidden.start()
        tile(0).start()

        def step(i):
            nt, kc = i // depth, i % depth
            tile(i).wait()

            @pl.when(i + 1 < steps)
            def _():
                tile(i + 1).start()

            @pl.when(kc == 0)
            def _():
                clear(acc)

            acc[...] += lax.dot_general(
                hid_v[pl.ds(pl.multiple_of(kc * TK, 8), TK), :], dy_v[i % 2], (((0,), (0,)), ((), ())), preferred_element_type=F32)

            @pl.when(kc == depth - 1)
            def _():
                @pl.when(nt > 0)
                def _():
                    result(nt - 1).wait()

                out_v[...] = acc[...].astype(BF16)
                result(nt).start()

        @pl.loop(A_END, B_END)
        def _(t):
            exchange(t, False)

            @pl.when(t == A_END)
            def _():
                hidden.wait()

            begin = (t - A_END) * per_tick
            spread(t, False, begin, jnp.minimum(begin + per_tick, steps), step)

        result(wide - 1).wait()

    pl.run_scoped(
        second,
        pltpu.VMEM((T, F), BF16), pltpu.VMEM((2, TK, TND), BF16), pltpu.VMEM((F, TND), F32), pltpu.VMEM((F, TND), BF16),
        pltpu.SemaphoreType.DMA, pltpu.SemaphoreType.DMA((2,)), pltpu.SemaphoreType.DMA,
    )

    def third(acc):
        def near(d_v, x_v, d_sem, x_sem):
            steps = D // TM2
            per_tick = -(-steps // (N_END - B_END))
            half = pl.ds(pl.multiple_of(y * 4 * B, 8), 4 * B)
            grads = [pltpu.make_async_copy(h.at[half], d_v.at[:, pl.ds(i * F, F)], d_sem.at[i]) for i, h in enumerate((dgs, dus))]

            def tile(i):
                return pltpu.make_async_copy(gx.at[half, pl.ds(pl.multiple_of(i * TM2, 128), TM2)], x_v.at[i % 2], x_sem.at[i % 2])

            def step(i):
                tile(i).wait()

                @pl.when(i + 1 < steps)
                def _():
                    tile(i + 1).start()

                acc[pl.ds(pl.multiple_of(i * TM2, 8), TM2), :] = lax.dot_general(
                    x_v[i % 2], d_v[...], (((0,), (0,)), ((), ())), preferred_element_type=F32)

            for copy in grads:
                copy.start()

            @pl.loop(B_END, N_END)
            def _(t):
                exchange(t, False)

                @pl.when(t == B_END)
                def _():
                    for q in range(4):
                        wait_sibling(1, y * 4 + q)
                    tile(0).start()
                    for copy in grads:
                        copy.wait()

                begin = (t - B_END) * per_tick
                spread(t, False, begin, jnp.minimum(begin + per_tick, steps), step)

        pl.run_scoped(
            near,
            pltpu.VMEM((4 * B, 2 * F), BF16), pltpu.VMEM((2, 4 * B, TM2), BF16),
            pltpu.SemaphoreType.DMA((2,)), pltpu.SemaphoreType.DMA((2,)),
        )

        def far(d_v, x_v, out_v, d_sem, x_sem, o_sem):
            wide = D // TM
            steps = wide * 4
            early = wide * 3
            per_tick = -(-early // (L_T - N_END))
            last_per_tick = -(-wide // 2)

            def block_of(m):
                return (1 - y) * 4 + order(m, z)

            def grads(m):
                at = block_of(m) * B
                return [
                    pltpu.make_async_copy(rows(h, at, B), d_v.at[m % 2, :, pl.ds(i * F, F)], d_sem.at[m % 2, i])
                    for i, h in enumerate((dgs, dus))
                ]

            def tile(i):
                return pltpu.make_async_copy(
                    gx.at[pl.ds(pl.multiple_of(block_of(i // wide) * B, 8), B), pl.ds(pl.multiple_of((i % wide) * TM, 128), TM)],
                    x_v.at[i % 2], x_sem.at[i % 2])

            def results(mt):
                at = pl.ds(pl.multiple_of(mt * TM, 8), TM)
                return [pltpu.make_async_copy(out_v.at[i], h.at[at], o_sem.at[i]) for i, h in enumerate((dwg, dwu))]

            def fetch(i):
                @pl.when(i % wide == 0)
                def _():
                    wait_sibling(1, block_of(i // wide))

                tile(i).start()

            def step(i):
                m, mt = i // wide, i % wide

                @pl.when(mt == 0)
                def _():
                    for copy in grads(m):
                        copy.wait()

                    @pl.when(m < 3)
                    def _():
                        for copy in grads(m + 1):
                            copy.start()

                tile(i).wait()

                @pl.when((i + 1 < steps) & (i + 1 != early))
                def _():
                    fetch(i + 1)

                at = pl.ds(pl.multiple_of(mt * TM, 8), TM)
                acc[at, :] += lax.dot_general(x_v[i % 2], d_v[m % 2], (((0,), (0,)), ((), ())), preferred_element_type=F32)

                @pl.when(m == 3)
                def _():
                    @pl.when(mt > 0)
                    def _():
                        for copy in results(mt - 1):
                            copy.wait()

                    for n in (0, 1):
                        out_v[n] = acc[at, pl.ds(n * F, F)].astype(BF16)
                    for copy in results(mt):
                        copy.start()

            for copy in grads(0):
                copy.start()

            @pl.loop(N_END, C_END)
            def _(t):
                exchange(t, True)

                @pl.when(t == N_END)
                def _():
                    fetch(0)

                @pl.when(t == L_T)
                def _():
                    fetch(early)

                def first_of(t):
                    return jnp.where(
                        t < L_T, jnp.minimum((t - N_END) * per_tick, early), jnp.minimum(early + (t - L_T) * last_per_tick, steps))

                spread(t, True, first_of(t), first_of(t + 1), step)

            for copy in results(wide - 1):
                copy.wait()

        pl.run_scoped(
            far,
            pltpu.VMEM((2, B, 2 * F), BF16), pltpu.VMEM((2, B, TM), BF16), pltpu.VMEM((2, TM, F), BF16),
            pltpu.SemaphoreType.DMA((2, 2)), pltpu.SemaphoreType.DMA((2,)), pltpu.SemaphoreType.DMA((2,)),
        )

    pl.run_scoped(third, pltpu.VMEM((D, 2 * F), F32))

    for t in range(C_END, C_END + KEEP):
        arrive_y(1, t, True)
        for d in (0, 1):
            sum_drain(d, t)
        y_drain(t)
    for a in (0, 1):
        own_to_sibling(a).wait_send()
    out = lambda j: pltpu.make_async_copy(out_b.at[j % 2, 0], rows(dx, j * C, C), load_sem.at[j % 2, 5])
    for j in (0, 1):
        end_loads(j % 2, j, False, True)
    for j in range(NC):
        b = j % 2
        end_loads(b, j, False, False)
        ref = rows(yin, j * C, C)
        pltpu.make_async_remote_copy(ref, ref, ry_send.at[0], ry_recv.at[j], **dev(1 - y, z, c)).wait_recv()
        last = pltpu.make_async_copy(ref, in_b.at[b, jnp.where(middle, 2, 1)], load_sem.at[b, 4])
        last.start()
        last.wait()
        if j >= 2:
            out(j - 2).wait()

        @pl.when(middle)
        def _(b=b):
            add(b, 0, 3)

        @pl.when(jnp.logical_not(middle))
        def _(b=b):
            add(b, 0, 2)

        out(j).start()
        if j + 2 < NC:
            end_loads(b, j + 2, False, True)
    for j in (NC - 2, NC - 1):
        out(j).wait()


def fused(dims, x, dy, gate, up, wg, wu, wd):
    R, D, F = dims[:3]
    C, T = R // NC, 2 * R * BLOCKS
    hbm = pl.BlockSpec(memory_space=pl.ANY)
    shape = jax.ShapeDtypeStruct
    outs = (
        shape((R, D), BF16), shape((D, F), BF16), shape((D, F), BF16), shape((F, D), BF16),
        shape((T, D), BF16), shape((T, D), BF16), shape((T // 2, D), F32), shape((T // 2, D), BF16),
        shape((2, 6 * R, D), BF16), shape((R, D), BF16),
        shape((T, F), BF16), shape((T, F), BF16), shape((T, F), BF16),
    )
    dma = pltpu.SemaphoreType.DMA
    results = pl.pallas_call(
        functools.partial(kernel, dims),
        out_shape=outs,
        in_specs=[hbm] * 7,
        out_specs=[hbm] * len(outs),
        scratch_shapes=[
            pltpu.VMEM((2, C, D), F32), pltpu.VMEM((2, C, D), BF16), pltpu.VMEM((2, 3, C, D), BF16), pltpu.VMEM((2, 3, C, D), BF16),
            dma((2, 2, 4)), dma((2, 2, 12)), dma((2, 4)), dma((2, 16)), dma((3, 2, 4)), dma((2, 8)), dma((2,)),
            dma((2, 3)), dma((2, 24)), dma((3,)), dma((NC,)), dma((BLOCKS,)), dma((2, 6)),
        ],
        compiler_params=pltpu.CompilerParams(collective_id=0, has_side_effects=True, vmem_limit_bytes=67043328),
        name="mlp_backward",
    )(x, dy, gate, up, wg, wu, wd)
    return handed_on(*results[:4])


def handed_on(*arrays):
    pieces = []
    for n, a in enumerate(arrays):
        count = next(k for k in (10, 8, 2) if a.shape[0] % (8 * k) == 0)
        pieces += [(n, i * (a.shape[0] // count), a.shape[0] // count) for i in range(count)]

    def kernel(*refs):
        ins, outs, held = refs[:4], refs[4:8], refs[8:12]
        sems = refs[12]

        def copy(way, i):
            n, at, high = pieces[i]
            part = pl.ds(at, high)
            src, dst = ((ins, held), (held, outs))[way]
            return pltpu.make_async_copy(src[n].at[part], dst[n].at[part], sems.at[way, i])

        for i in range(len(pieces)):
            copy(0, i).start()
        for i in range(len(pieces)):
            copy(0, i).wait()
            copy(1, i).start()
        for i in range(len(pieces)):
            copy(1, i).wait()

    hbm = pl.BlockSpec(memory_space=pl.ANY)
    return pl.pallas_call(
        kernel,
        out_shape=[jax.ShapeDtypeStruct(a.shape, a.dtype) for a in arrays],
        in_specs=[hbm] * 4,
        out_specs=[hbm] * 4,
        scratch_shapes=[pltpu.VMEM(a.shape, a.dtype) for a in arrays] + [pltpu.SemaphoreType.DMA((2, len(pieces)))],
        compiler_params=pltpu.CompilerParams(vmem_limit_bytes=67043328),
        name="hand_on",
    )(*arrays)


def solution(mesh):
    def step(x, dy, gate, up, wg, wu, wd):
        (rows, depth), wide = x.shape, wg.shape[1]
        dims = (rows, depth, wide, 512, 1024, 512, 256, 1280, 512, 1024)
        return fused(dims, x, dy, gate, up, wg, wu, wd)

    tokens, columns = P(("dp", "tp"), None), P("dp", "tp")
    return jax.shard_map(
        step,
        mesh=mesh,
        in_specs=(tokens, tokens, columns, columns, P(None, "tp"), P(None, "tp"), P("tp", None)),
        out_specs=(tokens, columns, columns, tokens),
        check_vma=False,
    )
```

time: 1120 us -> 482 us (0.43)
  waiting for transfers between devices: 538 us -> 0 us
  Pallas kernels: 0 us -> 481 us
  matrix products: 413 us -> 0 us
  starting transfers between devices: 73.5 us -> 0 us
  local copies, waits for them, and re-layouts: 35.9 us -> 0 us
  other arithmetic: 29.3 us -> 0 us
  between operations: 13.9 us -> 0.64 us
    pallas_call x0 -> x2, Pallas kernels: none -> 481 us  [the longest x1 457 us: fused(): pl.pallas_call(functools.partial(kernel, dims), out_shape=outs, in_specs=...]
    dot_general x13 -> x0, matrix products: 413 us -> none  [the longest x10 240 us: by_group(): jnp.einsum('gta,gtb->gab', a, b, preferred_element_type=jnp.float32)]
    dot_general x17 -> x0, waiting for transfers between devices: 352 us -> none  [by_group(): jnp.einsum('gta,gtb->gab', a, b, preferred_element_type=jnp.float32)]
    unnamed x5 -> x0, waiting for transfers between devices: 186 us -> none
    dot_general x17 -> x0, starting transfers between devices: 73.4 us -> none  [by_group(): jnp.einsum('gta,gtb->gab', a, b, preferred_element_type=jnp.float32)]
    unnamed x7 -> x0, local copies, waits for them, and re-layouts: 33.6 us -> none
    reshape x2 -> x0, other arithmetic: 29.3 us -> none  [the longest x1 17 us: by_group(): a, b = (t.reshape(groups, -1, t.shape[-1]) for t in (a, b))]
  transfers between devices with their start and end apart: 20 -> 0, of which waited for: 12 -> 0; matrix products, arithmetic and copies ran while one was open for 43% -> 0% of each run, Pallas kernels for 0% -> 0%
where the time goes in v1:
time: 482 us; the launch traced here: 481 us
  Pallas kernels  481 us (100%)
    pallas_call x1, Pallas kernels, fused(): pl.pallas_call(functools.partial(kernel, dims), out_shape=outs, in_specs=...  457 us
    pallas_call x1, Pallas kernels, handed_on(): pl.pallas_call(kernel, out_shape=[jax.ShapeDtypeStruct(a.shape, a.dtype)...  23.3 us

profile of v1, /device:TPU:0, one launch (start us, length us, event | category | flops | bytes accessed | tf_op | source)
XLA Modules:
  0.0 481.4 jit_solution(9981522567086183467)
XLA Ops:
  0.6 457.4 %mlp_backward.1 = (bf16[224,5120]{1,0:T(8,128)(2,1)}, bf16[5120,1024]{1,0:T(8,128)(2,1)}, bf16[5120,1024]{1,0:T(8,128)(2,1)}, bf16[1024,5120]{1,0:T(8,128)(2,1)}...) custom-call(bf16[224,5120]{1,0:T(8,128)(2,1)} %x.1, ...), custom_call_target="tpu_custom_call" | custom-call | tf_op jit(solution)/shard_map/mlp_backward/pallas_call | solution.py:779
  458.1 23.3 %hand_on.1 = (bf16[224,5120]{1,0:T(8,128)(2,1)}, bf16[5120,1024]{1,0:T(8,128)(2,1)}, bf16[5120,1024]{1,0:T(8,128)(2,1)}, bf16[1024,5120]{1,0:T(8,128)(2,1)}) custom-call(bf16[224,5120]{1,0:T(8,128)(2,1)} %get-tuple-element.8.refs_0_, bf16[5120,1024]{1,0:T(8,128)(2,1)} %get-tuple-element.9.refs_1_, bf16[5120,1024]{1,0:T(8,128)(2,1)} %get-tuple-element.10.refs_2_, ...), custom_call_target="tpu_custom_call" | custom-call | tf_op jit(solution)/shard_map/hand_on/pallas_call | solution.py:820

commit v2 on v1

--- a/solution.py
+++ b/solution.py
@@ -13,8 +13,9 @@
 BLOCKS = 8
 LAG = 2
 KEEP = 3
-Y_X, RS_Y = 16, 32
-A_END, B_END, N_END, L_T, C_END = 20, 25, 29, 33, 36
+Y_X = 16
+MINE, OTHERS = 26, 30
+A_END, B_END, N_END, T_END = 20, 25, 29, 34
 
 
 def order(p, z):
@@ -26,12 +27,12 @@
 def kernel(
     dims,
     x, dy, gate, up, wg, wu, wd,
-    dx, dwg, dwu, dwd, gx, gdy, own, sib, ins, yin, dgs, dus, hids,
+    ysum, mysum, dwd, part, gx, gdy, own, sib, ins, dgs, dus, hids,
     own_b, sib_b, in_b, out_b,
     z_send, z_recv, y_send, y_recv, sib_send, sib_recv, own_send,
-    rs_send, rs_recv, ry_send, ry_recv, dxs_recv, load_sem,
+    rs_send, rs_recv, dxs_recv, load_sem, end_sem,
 ):
-    R, D, F, TF, TN, TM, TM2, TND, TK, TV = dims
+    R, D, F, TF, TN, TM, TND, TK, TV = dims
     C, B, T = R // NC, 2 * R, 2 * R * BLOCKS
     dp, tp = lax.axis_index("dp"), lax.axis_index("tp")
     y, z, c = tp // 8, (tp // 2) % 4, tp % 2
@@ -131,7 +132,7 @@
         def _():
             copy(t).start()
 
-    def arrive_y(a, t, drain_only=False):
+    def arrive_y(a, t):
         base = a * Y_X + LAG
 
         def chunk(t):
@@ -146,9 +147,6 @@
         def _():
             _, ref, idx = chunk(t - KEEP)
             to_sibling(a, ref, idx, sib_send.at[2, a, (t - KEEP) % 4]).wait_send()
-
-        if drain_only:
-            return
 
         @pl.when(active(t))
         def _():
@@ -190,19 +188,18 @@
             total = own_b[b, :, cols] + sib_b[b, :, cols].astype(F32)
             for m in range(n):
                 total = total + in_b[b, m, :, cols].astype(F32)
-            out_b[b, slot, :, cols] = total.astype(BF16)
+            if slot is None:
+                own_b[b, :, cols] = total
+            else:
+                out_b[b, slot, :, cols] = total.astype(BF16)
 
     def sum_state(d, t):
         pos, nxt = step_of(d)
-        base = jnp.where(pos == 0, 9, jnp.where(pos == 1, 11, 16))
-        first = jnp.where(pos == 0, 0, 2)
-        last = jnp.where(pos == 2, 4, 6)
-        on = (pos < 3) & (t >= base + NC * first) & (t < base + NC * last)
-        u = jnp.clip(t - base, 0, 23)
+        on = (pos < 3) & (t >= 8 + 8 * pos) & (t < 32)
+        u = jnp.clip(t - 8 - 4 * pos, 0, 23)
         k, j = u // NC, u % NC
-        to_pos = jnp.where(k < 2, 1, jnp.where(k < 4, 3, 2))
-        other = (k == 1) | (k == 3) | (k == 4)
-        idx = jnp.where(other, 1 - y, y) * 4 + z_at(d, to_pos)
+        to_pos = jnp.where(k < 3, k + 1, 6 - k)
+        idx = jnp.where(k < 3, y, 1 - y) * 4 + z_at(d, to_pos)
         return on, pos, nxt, k, j, idx
 
     def sum_send(d, t, nxt, k, j):
@@ -254,70 +251,64 @@
 
             sum_send(d, t, nxt, k, j).start()
 
-    def last_in(pos, other):
-        if other:
-            return jnp.where(pos == 1, 1, jnp.where(pos == 2, 4, 3))
-        return jnp.where(pos == 1, 0, jnp.where(pos == 2, 5, 2))
-
-    def end_loads(b, j, other, start):
+    end, middle = 2, (z > 0) & (z < 3)
+
+    def end_loads(other, j, start):
         idx = jnp.where(other, 1 - y, y) * 4 + z
         if start:
             @pl.when(j == 0)
             def _():
                 wait_partial(idx)
 
-        copies = [own_load(b, idx, j), sib_load(b, idx, j)]
-        for copy in copies:
+        for copy in (own_load(end, idx, j), sib_load(end, idx, j)):
             copy.start() if start else copy.wait()
         for d, there, slot in ((0, z > 0, 0), (1, z < 3, jnp.where(z > 0, 1, 0))):
             pos, _ = step_of(d)
-            k = last_in(pos, other)
+            k = jnp.where(other, 6 - pos, pos - 1)
 
             @pl.when(there)
             def _(d=d, k=k, slot=slot):
                 if start:
                     wait_in(d, k, j)
-                    in_load(b, slot, d, k, j).start()
+                    in_load(end, slot, d, k, j).start()
                 else:
-                    in_load(b, slot, d, k, j).wait()
-
-    middle = (z > 0) & (z < 3)
-    y_set = jnp.where(z < 2, 1, 0)
-
-    def y_copy(t):
-        j = jnp.clip(t - RS_Y, 0, NC - 1)
-        return pltpu.make_async_remote_copy(
-            out_b.at[y_set, t % 3], rows(yin, j * C, C), ry_send.at[t % 3], ry_recv.at[j], **dev(1 - y, z, c))
-
-    def y_on(t):
-        return (t >= RS_Y) & (t < RS_Y + NC)
-
-    def y_drain(t):
-        @pl.when(y_on(t - KEEP))
-        def _():
-            y_copy(t - KEEP).wait_send()
-
-    def y_loads(t):
-        @pl.when(y_on(t))
-        def _():
-            end_loads(y_set, t - RS_Y, True, True)
-
-    def y_sum(t):
-        y_drain(t)
-
-        @pl.when(y_on(t))
-        def _():
-            end_loads(y_set, t - RS_Y, True, False)
-
-            @pl.when(middle)
-            def _():
-                add(y_set, t % 3, 2)
-
-            @pl.when(jnp.logical_not(middle))
-            def _():
-                add(y_set, t % 3, 1)
-
-            y_copy(t).start()
+                    in_load(end, slot, d, k, j).wait()
+
+    def end_state(t):
+        other = t >= OTHERS
+        return (t >= MINE) & (t < OTHERS + NC), other, jnp.clip(jnp.where(other, t - OTHERS, t - MINE), 0, NC - 1)
+
+    def end_store(t, start):
+        on, other, j = end_state(t)
+        for mine in (True, False):
+            @pl.when(on & (other != mine))
+            def _(mine=mine):
+                src, dst = (own_b.at[end], mysum) if mine else (out_b.at[end, 0], ysum)
+                copy = pltpu.make_async_copy(src, rows(dst, j * C, C), end_sem)
+                copy.start() if start else copy.wait()
+
+    def last_loads(t):
+        end_store(t - 1, False)
+        on, other, j = end_state(t)
+
+        @pl.when(on)
+        def _():
+            end_loads(other, j, True)
+
+    def last_sum(t):
+        on, other, j = end_state(t)
+
+        @pl.when(on)
+        def _():
+            end_loads(other, j, False)
+
+        for mine in (True, False):
+            for n, where in ((2, middle), (1, jnp.logical_not(middle))):
+                @pl.when(on & (other != mine) & where)
+                def _(mine=mine, n=n):
+                    add(end, None if mine else 0, n)
+
+        end_store(t, True)
 
     def clear(ref):
         high = min(64, ref.shape[0])
@@ -338,13 +329,13 @@
         for d in (0, 1):
             sum_loads(d, t)
         if late:
-            y_loads(t)
+            last_loads(t)
 
     def sums(t, late):
         for d in (0, 1):
             sum_add(d, t)
         if late:
-            y_sum(t)
+            last_sum(t)
 
     def spread(t, late, begin, end, step):
         @pl.loop(0, jnp.maximum(end - begin, 2))
@@ -377,8 +368,9 @@
         weights = [pltpu.make_async_copy(h, v, w_sem.at[i]) for i, (h, v) in enumerate(((wd, wd_v), (wg, wg_v), (wu, wu_v)))]
 
         def block_of(n):
-            other = (n // 2) % 2
-            return jnp.where(other == 1, 1 - y, y) * 4 + order(n % 2 + 2 * (n // 4), z)
+            other = (n == 2) | (n == 4) | (n >= 6)
+            p = jnp.where(other, jnp.where(n == 7, 3, n // 2 - 1), jnp.where(n < 2, n, (n + 1) // 2))
+            return jnp.where(other, 1 - y, y) * 4 + order(p, z)
 
         def gate_up(n):
             at = block_of(n) * B
@@ -414,8 +406,8 @@
         def drain(n):
             for copy in kept_grads(n):
                 copy.wait()
-            for slot in (0, 1):
-                wait_terms(n, tiles - 2 + slot, slot)
+            for tile in (tiles - 2, tiles - 1):
+                wait_terms(n, tile, tile % 2)
 
         def gradients(n):
             @pl.when(n == 0)
@@ -472,6 +464,8 @@
                 mine.start()
                 theirs.start()
 
+            drain(n)
+
         @pl.loop(0, A_END)
         def _(t):
             exchange(t, False)
@@ -500,10 +494,6 @@
                 load = pltpu.make_async_copy(rows(gdy, idx * B, B), dy_v, dy_sem)
                 load.start()
 
-                @pl.when(n > 0)
-                def _():
-                    drain(n - 1)
-
                 sums(t, False)
                 load.wait()
                 gradients(n)
@@ -511,8 +501,6 @@
             @pl.when((t == 3) | ((t >= 7) & (t % 2 == 1)))
             def _():
                 dx_terms(t, n)
-
-        drain(BLOCKS - 1)
 
     pl.run_scoped(
         first,
@@ -585,253 +573,180 @@
         pltpu.SemaphoreType.DMA, pltpu.SemaphoreType.DMA((2,)), pltpu.SemaphoreType.DMA,
     )
 
-    def third(acc):
-        def near(d_v, x_v, d_sem, x_sem):
-            steps = D // TM2
-            per_tick = -(-steps // (N_END - B_END))
-            half = pl.ds(pl.multiple_of(y * 4 * B, 8), 4 * B)
-            grads = [pltpu.make_async_copy(h.at[half], d_v.at[:, pl.ds(i * F, F)], d_sem.at[i]) for i, h in enumerate((dgs, dus))]
-
-            def tile(i):
-                return pltpu.make_async_copy(gx.at[half, pl.ds(pl.multiple_of(i * TM2, 128), TM2)], x_v.at[i % 2], x_sem.at[i % 2])
-
-            def step(i):
-                tile(i).wait()
-
-                @pl.when(i + 1 < steps)
-                def _():
-                    tile(i + 1).start()
-
-                acc[pl.ds(pl.multiple_of(i * TM2, 8), TM2), :] = lax.dot_general(
-                    x_v[i % 2], d_v[...], (((0,), (0,)), ((), ())), preferred_element_type=F32)
-
-            for copy in grads:
-                copy.start()
-
-            @pl.loop(B_END, N_END)
-            def _(t):
-                exchange(t, False)
-
-                @pl.when(t == B_END)
-                def _():
-                    for q in range(4):
-                        wait_sibling(1, y * 4 + q)
-                    tile(0).start()
-                    for copy in grads:
-                        copy.wait()
-
-                begin = (t - B_END) * per_tick
-                spread(t, False, begin, jnp.minimum(begin + per_tick, steps), step)
-
-        pl.run_scoped(
-            near,
-            pltpu.VMEM((4 * B, 2 * F), BF16), pltpu.VMEM((2, 4 * B, TM2), BF16),
-            pltpu.SemaphoreType.DMA((2,)), pltpu.SemaphoreType.DMA((2,)),
-        )
-
-        def far(d_v, x_v, out_v, d_sem, x_sem, o_sem):
-            wide = D // TM
-            steps = wide * 4
-            early = wide * 3
-            per_tick = -(-early // (L_T - N_END))
-            last_per_tick = -(-wide // 2)
-
-            def block_of(m):
-                return (1 - y) * 4 + order(m, z)
-
-            def grads(m):
-                at = block_of(m) * B
-                return [
-                    pltpu.make_async_copy(rows(h, at, B), d_v.at[m % 2, :, pl.ds(i * F, F)], d_sem.at[m % 2, i])
-                    for i, h in enumerate((dgs, dus))
-                ]
-
-            def tile(i):
-                return pltpu.make_async_copy(
-                    gx.at[pl.ds(pl.multiple_of(block_of(i // wide) * B, 8), B), pl.ds(pl.multiple_of((i % wide) * TM, 128), TM)],
-                    x_v.at[i % 2], x_sem.at[i % 2])
-
-            def results(mt):
-                at = pl.ds(pl.multiple_of(mt * TM, 8), TM)
-                return [pltpu.make_async_copy(out_v.at[i], h.at[at], o_sem.at[i]) for i, h in enumerate((dwg, dwu))]
-
-            def fetch(i):
-                @pl.when(i % wide == 0)
-                def _():
-                    wait_sibling(1, block_of(i // wide))
-
-                tile(i).start()
-
-            def step(i):
-                m, mt = i // wide, i % wide
-
-                @pl.when(mt == 0)
-                def _():
-                    for copy in grads(m):
-                        copy.wait()
-
-                    @pl.when(m < 3)
-                    def _():
-                        for copy in grads(m + 1):
-                            copy.start()
-
-                tile(i).wait()
-
-                @pl.when((i + 1 < steps) & (i + 1 != early))
-                def _():
-                    fetch(i + 1)
-
-                at = pl.ds(pl.multiple_of(mt * TM, 8), TM)
-                acc[at, :] += lax.dot_general(x_v[i % 2], d_v[m % 2], (((0,), (0,)), ((), ())), preferred_element_type=F32)
-
-                @pl.when(m == 3)
-                def _():
-                    @pl.when(mt > 0)
-                    def _():
-                        for copy in results(mt - 1):
-                            copy.wait()
-
-                    for n in (0, 1):
-                        out_v[n] = acc[at, pl.ds(n * F, F)].astype(BF16)
-                    for copy in results(mt):
-                        copy.start()
-
-            for copy in grads(0):
-                copy.start()
-
-            @pl.loop(N_END, C_END)
-            def _(t):
-                exchange(t, True)
-
-                @pl.when(t == N_END)
-                def _():
-                    fetch(0)
-
-                @pl.when(t == L_T)
-                def _():
-                    fetch(early)
-
-                def first_of(t):
-                    return jnp.where(
-                        t < L_T, jnp.minimum((t - N_END) * per_tick, early), jnp.minimum(early + (t - L_T) * last_per_tick, steps))
-
-                spread(t, True, first_of(t), first_of(t + 1), step)
-
-            for copy in results(wide - 1):
-                copy.wait()
-
-        pl.run_scoped(
-            far,
-            pltpu.VMEM((2, B, 2 * F), BF16), pltpu.VMEM((2, B, TM), BF16), pltpu.VMEM((2, TM, F), BF16),
-            pltpu.SemaphoreType.DMA((2, 2)), pltpu.SemaphoreType.DMA((2,)), pltpu.SemaphoreType.DMA((2,)),
-        )
-
-    pl.run_scoped(third, pltpu.VMEM((D, 2 * F), F32))
-
-    for t in range(C_END, C_END + KEEP):
-        arrive_y(1, t, True)
-        for d in (0, 1):
-            sum_drain(d, t)
-        y_drain(t)
+    def third(d_v, x_v, out_v, d_sem, x_sem, o_sem):
+        steps = D // TM
+        per_tick = -(-steps // (N_END - B_END))
+        half = pl.ds(pl.multiple_of(y * 4 * B, 8), 4 * B)
+        grads = [pltpu.make_async_copy(h.at[half], d_v.at[:, pl.ds(i * F, F)], d_sem.at[i]) for i, h in enumerate((dgs, dus))]
+
+        def tile(i):
+            return pltpu.make_async_copy(gx.at[half, pl.ds(pl.multiple_of(i * TM, 128), TM)], x_v.at[i % 2], x_sem.at[i % 2])
+
+        def result(i):
+            return pltpu.make_async_copy(out_v.at[i % 2], part.at[pl.ds(pl.multiple_of(i * TM, 8), TM)], o_sem.at[i % 2])
+
+        def step(i):
+            tile(i).wait()
+
+            @pl.when(i + 1 < steps)
+            def _():
+                tile(i + 1).start()
+
+            @pl.when(i >= 2)
+            def _():
+                result(i - 2).wait()
+
+            out_v[i % 2] = lax.dot_general(x_v[i % 2], d_v[...], (((0,), (0,)), ((), ())), preferred_element_type=F32)
+            result(i).start()
+
+        for copy in grads:
+            copy.start()
+
+        @pl.loop(B_END, N_END)
+        def _(t):
+            exchange(t, True)
+
+            @pl.when(t == B_END)
+            def _():
+                for q in range(4):
+                    wait_sibling(1, y * 4 + q)
+                tile(0).start()
+                for copy in grads:
+                    copy.wait()
+
+            begin = (t - B_END) * per_tick
+            spread(t, True, begin, jnp.minimum(begin + per_tick, steps), step)
+
+        for i in (steps - 2, steps - 1):
+            result(i).wait()
+
+    pl.run_scoped(
+        third,
+        pltpu.VMEM((4 * B, 2 * F), BF16), pltpu.VMEM((2, 4 * B, TM), BF16), pltpu.VMEM((2, TM, 2 * F), F32),
+        pltpu.SemaphoreType.DMA((2,)), pltpu.SemaphoreType.DMA((2,)), pltpu.SemaphoreType.DMA((2,)),
+    )
+
+    @pl.loop(N_END, T_END + KEEP)
+    def _(t):
+        exchange(t, True)
+        sums(t, True)
+
+    for q in range(4):
+        wait_sibling(1, (1 - y) * 4 + q)
     for a in (0, 1):
         own_to_sibling(a).wait_send()
-    out = lambda j: pltpu.make_async_copy(out_b.at[j % 2, 0], rows(dx, j * C, C), load_sem.at[j % 2, 5])
-    for j in (0, 1):
-        end_loads(j % 2, j, False, True)
-    for j in range(NC):
-        b = j % 2
-        end_loads(b, j, False, False)
-        ref = rows(yin, j * C, C)
-        pltpu.make_async_remote_copy(ref, ref, ry_send.at[0], ry_recv.at[j], **dev(1 - y, z, c)).wait_recv()
-        last = pltpu.make_async_copy(ref, in_b.at[b, jnp.where(middle, 2, 1)], load_sem.at[b, 4])
-        last.start()
-        last.wait()
-        if j >= 2:
-            out(j - 2).wait()
-
-        @pl.when(middle)
-        def _(b=b):
-            add(b, 0, 3)
-
-        @pl.when(jnp.logical_not(middle))
-        def _(b=b):
-            add(b, 0, 2)
-
-        out(j).start()
-        if j + 2 < NC:
-            end_loads(b, j + 2, False, True)
-    for j in (NC - 2, NC - 1):
-        out(j).wait()
+
+
+def finish_kernel(dims, part, gx, dgs, dus, down, dwg, dwu, dwd, d_v, x_v, p_v, out_v, down_v, d_sem, x_sem, p_sem, o_sem, c_sem):
+    R, D, F, TM = dims[0], dims[1], dims[2], dims[5]
+    steps, depth = D // TM, gx.shape[0] // 2
+    half = pl.ds(pl.multiple_of((1 - lax.axis_index("tp") // 8) * depth, 8), depth)
+    grads = [pltpu.make_async_copy(h.at[half], d_v.at[:, pl.ds(i * F, F)], d_sem.at[i]) for i, h in enumerate((dgs, dus))]
+    pieces, high = 8, F // 8
+
+    def tiles(i):
+        at = pl.multiple_of(i * TM, 128)
+        return [
+            pltpu.make_async_copy(gx.at[half, pl.ds(at, TM)], x_v.at[i % 2], x_sem.at[i % 2]),
+            pltpu.make_async_copy(part.at[pl.ds(at, TM)], p_v.at[i % 2], p_sem.at[i % 2]),
+        ]
+
+    def results(i):
+        at = pl.ds(pl.multiple_of(i * TM, 8), TM)
+        return [pltpu.make_async_copy(out_v.at[i % 2, n], h.at[at], o_sem.at[i % 2, n]) for n, h in enumerate((dwg, dwu))]
+
+    def piece(way, i):
+        at = pl.ds(pl.multiple_of(i * high, 8), high)
+        if way == 0:
+            return pltpu.make_async_copy(down.at[at], down_v.at[at], c_sem.at[0, i])
+        return pltpu.make_async_copy(down_v.at[at], dwd.at[at], c_sem.at[1, i])
+
+    for copy in grads + tiles(0):
+        copy.start()
+    for copy in grads:
+        copy.wait()
+    for i in range(pieces):
+        piece(0, i).start()
+
+    @pl.loop(0, steps)
+    def _(i):
+        for copy in tiles(i):
+            copy.wait()
+
+        @pl.when(i + 1 < steps)
+        def _():
+            for copy in tiles(i + 1):
+                copy.start()
+
+        @pl.when(i < pieces)
+        def _():
+            piece(0, i).wait()
+            piece(1, i).start()
+
+        @pl.when(i >= 2)
+        def _():
+            for copy in results(i - 2):
+                copy.wait()
+
+        p_v[i % 2] += lax.dot_general(x_v[i % 2], d_v[...], (((0,), (0,)), ((), ())), preferred_element_type=F32)
+        for n in (0, 1):
+            out_v[i % 2, n] = p_v[i % 2, :, pl.ds(n * F, F)].astype(BF16)
+        for copy in results(i):
+            copy.start()
+
+    for i in (steps - 2, steps - 1):
+        for copy in results(i):
+            copy.wait()
+    for i in range(pieces):
+        piece(1, i).wait()
 
 
 def fused(dims, x, dy, gate, up, wg, wu, wd):
-    R, D, F = dims[:3]
+    R, D, F, TM = dims[0], dims[1], dims[2], dims[5]
     C, T = R // NC, 2 * R * BLOCKS
     hbm = pl.BlockSpec(memory_space=pl.ANY)
-    shape = jax.ShapeDtypeStruct
+    shape, vmem, dma = jax.ShapeDtypeStruct, pltpu.VMEM, pltpu.SemaphoreType.DMA
     outs = (
-        shape((R, D), BF16), shape((D, F), BF16), shape((D, F), BF16), shape((F, D), BF16),
+        shape((R, D), BF16), shape((R, D), F32), shape((F, D), BF16), shape((D, 2 * F), F32),
         shape((T, D), BF16), shape((T, D), BF16), shape((T // 2, D), F32), shape((T // 2, D), BF16),
-        shape((2, 6 * R, D), BF16), shape((R, D), BF16),
-        shape((T, F), BF16), shape((T, F), BF16), shape((T, F), BF16),
+        shape((2, 6 * R, D), BF16), shape((T, F), BF16), shape((T, F), BF16), shape((T, F), BF16),
     )
-    dma = pltpu.SemaphoreType.DMA
-    results = pl.pallas_call(
+    product = 2 * T * D * F
+    ysum, mysum, down, part, gx, _, _, _, _, dgs, dus, _ = pl.pallas_call(
         functools.partial(kernel, dims),
         out_shape=outs,
         in_specs=[hbm] * 7,
         out_specs=[hbm] * len(outs),
         scratch_shapes=[
-            pltpu.VMEM((2, C, D), F32), pltpu.VMEM((2, C, D), BF16), pltpu.VMEM((2, 3, C, D), BF16), pltpu.VMEM((2, 3, C, D), BF16),
+            vmem((3, C, D), F32), vmem((3, C, D), BF16), vmem((3, 2, C, D), BF16), vmem((3, 3, C, D), BF16),
             dma((2, 2, 4)), dma((2, 2, 12)), dma((2, 4)), dma((2, 16)), dma((3, 2, 4)), dma((2, 8)), dma((2,)),
-            dma((2, 3)), dma((2, 24)), dma((3,)), dma((NC,)), dma((BLOCKS,)), dma((2, 6)),
+            dma((2, 3)), dma((2, 24)), dma((BLOCKS,)), dma((3, 4)), dma,
         ],
         compiler_params=pltpu.CompilerParams(collective_id=0, has_side_effects=True, vmem_limit_bytes=67043328),
+        cost_estimate=pl.CostEstimate(flops=5 * product, bytes_accessed=10 * T * D, transcendentals=0),
         name="mlp_backward",
     )(x, dy, gate, up, wg, wu, wd)
-    return handed_on(*results[:4])
-
-
-def handed_on(*arrays):
-    pieces = []
-    for n, a in enumerate(arrays):
-        count = next(k for k in (10, 8, 2) if a.shape[0] % (8 * k) == 0)
-        pieces += [(n, i * (a.shape[0] // count), a.shape[0] // count) for i in range(count)]
-
-    def kernel(*refs):
-        ins, outs, held = refs[:4], refs[4:8], refs[8:12]
-        sems = refs[12]
-
-        def copy(way, i):
-            n, at, high = pieces[i]
-            part = pl.ds(at, high)
-            src, dst = ((ins, held), (held, outs))[way]
-            return pltpu.make_async_copy(src[n].at[part], dst[n].at[part], sems.at[way, i])
-
-        for i in range(len(pieces)):
-            copy(0, i).start()
-        for i in range(len(pieces)):
-            copy(0, i).wait()
-            copy(1, i).start()
-        for i in range(len(pieces)):
-            copy(1, i).wait()
-
-    hbm = pl.BlockSpec(memory_space=pl.ANY)
-    return pl.pallas_call(
-        kernel,
-        out_shape=[jax.ShapeDtypeStruct(a.shape, a.dtype) for a in arrays],
-        in_specs=[hbm] * 4,
-        out_specs=[hbm] * 4,
-        scratch_shapes=[pltpu.VMEM(a.shape, a.dtype) for a in arrays] + [pltpu.SemaphoreType.DMA((2, len(pieces)))],
+    across = lax.ppermute(ysum, "tp", [(i, (i + 8) % 16) for i in range(16)])
+    weights = pl.pallas_call(
+        functools.partial(finish_kernel, dims),
+        out_shape=(shape((D, F), BF16), shape((D, F), BF16), shape((F, D), BF16)),
+        in_specs=[hbm] * 5,
+        out_specs=[hbm] * 3,
+        scratch_shapes=[
+            vmem((T // 2, 2 * F), BF16), vmem((2, T // 2, TM), BF16), vmem((2, TM, 2 * F), F32), vmem((2, 2, TM, F), BF16),
+            vmem((F, D), BF16), dma((2,)), dma((2,)), dma((2,)), dma((2, 2)), dma((2, 8)),
+        ],
         compiler_params=pltpu.CompilerParams(vmem_limit_bytes=67043328),
-        name="hand_on",
-    )(*arrays)
+        cost_estimate=pl.CostEstimate(flops=product, bytes_accessed=6 * T * D, transcendentals=0),
+        name="finish",
+    )(part, gx, dgs, dus, down)
+    return ((mysum + across.astype(F32)).astype(BF16), *weights)
 
 
 def solution(mesh):
     def step(x, dy, gate, up, wg, wu, wd):
         (rows, depth), wide = x.shape, wg.shape[1]
-        dims = (rows, depth, wide, 512, 1024, 512, 256, 1280, 512, 1024)
+        dims = (rows, depth, wide, 512, 1024, 256, 1280, 512, 1024)
         return fused(dims, x, dy, gate, up, wg, wu, wd)
 
     tokens, columns = P(("dp", "tp"), None), P("dp", "tp")

time: 482 us -> 466 us (0.967)
  Pallas kernels: 481 us -> 457 us
  other arithmetic: 0 us -> 5 us
    pallas_call x1, Pallas kernels: 457 us -> 404 us  [fused(): pl.pallas_call(functools.partial(kernel, dims), out_shape=outs, in_specs=...]
    pallas_call x1, Pallas kernels: 23.3 us -> 53.7 us  [fused(): pl.pallas_call(functools.partial(finish_kernel, dims), out_shape=(shape((...]
    convert_element_type x0 -> x1, other arithmetic: none -> 5 us  [fused(): return ((mysum + across.astype(F32)).astype(BF16), *weights)]
  transfers between devices with their start and end apart: 0 -> 1, of which waited for: 0 -> 0; matrix products, arithmetic and copies ran while one was open for 0% -> 0% of each run, Pallas kernels for 0% -> 12%
where the time goes in v2:
time: 466 us; the launch traced here: 464 us
  Pallas kernels  457 us (98%)
  other arithmetic  5 us (1%)
    pallas_call x1, Pallas kernels, fused(): pl.pallas_call(functools.partial(kernel, dims), out_shape=outs, in_specs=...  404 us
    pallas_call x1, Pallas kernels, fused(): pl.pallas_call(functools.partial(finish_kernel, dims), out_shape=(shape((...  53.7 us
  transfers between devices with their start and end apart: 1, of which 0 were waited for; matrix products, arithmetic and copies ran while one was open for 0% of the time, Pallas kernels for 12%

profile of v2, /device:TPU:0, one launch (start us, length us, event | category | flops | bytes accessed | tf_op | source)
XLA Modules:
  0.0 464.2 jit_solution(14733680028401010329)
XLA Ops:
  0.6 403.7 %mlp_backward.1 = (bf16[224,5120]{1,0:T(8,128)(2,1)}, f32[224,5120]{1,0:T(8,128)}, bf16[1024,5120]{1,0:T(8,128)(2,1)}, f32[5120,2048]{1,0:T(8,128)}, bf16[3584,5...) custom-call(bf16[224,5120]{1,0:T(8,128)(2,1)} %x.1, ...), custom_call_target="tpu_custom_call" | custom-call | flops 187904819200 | bytes 183500800 | tf_op jit(solution)/shard_map/mlp_backward/pallas_call | solution.py:715
  404.3 1.2 collective-permute-start
  405.5 53.7 %finish.1 = (bf16[5120,1024]{1,0:T(8,128)(2,1)}, bf16[5120,1024]{1,0:T(8,128)(2,1)}, bf16[1024,5120]{1,0:T(8,128)(2,1)}) custom-call(f32[5120,2048]{1,0:T(8,128)} %get-tuple-element.16.part, bf16[3584,5120]{1,0:T(8,128)(2,1)} %get-tuple-element.17.gx, bf16[3584,1024]{1,0:T(8,128)(2,1)} %get-tuple-element.18.dgs, bf16[3584,1024]{1,0:T(8,128)(2,1)} %get-tuple-element.19.dus, ...), custom_call_target="tpu_custom_call" | custom-call | flops 37580963840 | bytes 110100480 | tf_op jit(solution)/shard_map/finish/pallas_call | solution.py:730
  459.2 0.0 collective-permute-done
  459.2 5.0 %add_convert_fusion = bf16[224,5120]{1,0:T(8,128)(2,1)} fusion(f32[224,5120]{1,0:T(8,128)} %get-tuple-element.14, bf16[224,5120]{1,0:T(8,128)(2,1)} %collective-permute-done), kind=kLoop, calls=%fused_computation | loop fusion | flops 3440640 | bytes 9175040 | tf_op jit(solution)/shard_map/convert_element_type | solution.py:743
Async XLA Ops:
  404.3 54.9 %collective-permute-start = (bf16[224,5120]{1,0:T(8,128)(2,1)}, bf16[224,5120]{1,0:T(8,128)(2,1)}, u32[]{:S(2)}, u32[]{:S(2)}) collective-permute-start(bf16[224,5120]{1,0:T(8,128)(2,1)} %get-tuple-element.15), channel_id=1, source_target_pairs={{0,8},{1,9},{2,10},{3,11},{4,12},{5,13},{6,14},{7,15},{8,0},{9,1},... | collective-permute-start | bytes 6881288 | tf_op jit(solution)/shard_map/ppermute | solution.py:729

commit v3 on v2

--- a/solution.py
+++ b/solution.py
@@ -13,9 +13,12 @@
 BLOCKS = 8
 LAG = 2
 KEEP = 3
-Y_X = 16
-MINE, OTHERS = 26, 30
-A_END, B_END, N_END, T_END = 20, 25, 29, 34
+LATE = 3
+Y_X, Y_X3 = 16, 20
+CUT = 21
+SUMS = 11
+PARTS, OTHERS = 16, 28
+A_END, B_END, N_END, T_END = 19, 25, 29, 33
 
 
 def order(p, z):
@@ -27,12 +30,12 @@
 def kernel(
     dims,
     x, dy, gate, up, wg, wu, wd,
-    ysum, mysum, dwd, part, gx, gdy, own, sib, ins, dgs, dus, hids,
+    ysum, mysum, next_sum, back_sum, dwd, part, gx, gdy, own, sib, ins, dgs, dus, hids,
     own_b, sib_b, in_b, out_b,
-    z_send, z_recv, y_send, y_recv, sib_send, sib_recv, own_send,
+    z_send, z_recv, y_send, y_recv, short_send, sib_send, sib_recv, sib_short, own_send, cut_send, cut_recv, cut_sib,
     rs_send, rs_recv, dxs_recv, load_sem, end_sem,
 ):
-    R, D, F, TF, TN, TM, TND, TK, TV = dims
+    R, D, F, TF, TN, TM, TND, TK, TV, CUT_ROWS = dims
     C, B, T = R // NC, 2 * R, 2 * R * BLOCKS
     dp, tp = lax.axis_index("dp"), lax.axis_index("tp")
     y, z, c = tp // 8, (tp // 2) % 4, tp % 2
@@ -107,53 +110,93 @@
                 ref, ref, z_send.at[d, a, 0], z_recv.at[d, a, r], **dev(y, z, 1 - c)).wait_recv()
             to_sibling(a, ref, idx, sib_send.at[d, a, t % 4]).start()
 
-    def gather_y(a, t):
-        base = a * Y_X
-
+    def y_chunk(a, t, short):
+        if a == 0:
+            s = jnp.clip(t, 0, 4 * NC - 1)
+            return (t >= 0) & (t < 4 * NC), s // NC, s % NC, C
+        v = jnp.clip(t - Y_X3, 0, 9)
+        if short:
+            return (t > Y_X3) & (t <= Y_X3 + 9) & (v % 3 == 0), jnp.maximum(v // 3, 1), 3, C - CUT_ROWS
+        near = t < Y_X3
+        return (t >= Y_X) & (t < Y_X3 + 9), jnp.where(near, 0, 1 + v // 3), jnp.where(near, jnp.clip(t - Y_X, 0, 3), v % 3), C
+
+    def y_sems(a, t, short):
+        return (short_send.at[(t // 3) % 2], sib_short.at[(t // 3) % 2]) if short else (y_send.at[a, t % 4], sib_send.at[2, a, t % 4])
+
+    def gather_y(a, t, short=False):
         def copy(t, own_rows=False):
-            s = jnp.clip(t - base, 0, 15)
-            there = rows(kept[a], place(y, order(s // NC, z), c) + (s % NC) * C, C)
-            src = rows(sent[a], (s % NC) * C, C) if own_rows else there
-            return pltpu.make_async_remote_copy(
-                src, there, y_send.at[a, t % 4], y_recv.at[a, s], **dev(1 - y, z, c))
-
-        def active(t):
-            return (t >= base) & (t < base + 4 * NC)
-
-        @pl.when(active(t - KEEP))
+            _, p, j, high = y_chunk(a, t, short)
+            there = rows(kept[a], place(y, order(p, z), c) + j * C, high)
+            src = rows(sent[a], j * C, high) if own_rows else there
+            return pltpu.make_async_remote_copy(src, there, y_sems(a, t, short)[0], y_recv.at[a, p * NC + j], **dev(1 - y, z, c))
+
+        was, (on, p, _, _) = y_chunk(a, t - KEEP, short)[0], y_chunk(a, t, short)
+
+        @pl.when(was)
         def _():
             copy(t - KEEP).wait_send()
 
-        @pl.when(active(t) & (t < base + NC))
-        def _():
-            copy(t, True).start()
-
-        @pl.when(active(t) & (t >= base + NC))
+        if not short:
+            @pl.when(on & (p == 0))
+            def _():
+                copy(t, True).start()
+
+        @pl.when(on & (p > 0))
         def _():
             copy(t).start()
 
-    def arrive_y(a, t):
-        base = a * Y_X + LAG
+    def arrive_y(a, t, short=False):
+        def sent_at(t):
+            if a == 0:
+                return t - LAG
+            return jnp.where(t < Y_X3 + LAG, t - LAG, jnp.where(t < Y_X3 + LATE, -1, t - LATE))
 
         def chunk(t):
-            r = jnp.clip(t - base, 0, 15)
-            q = order(r // NC, z)
-            return r, rows(kept[a], place(1 - y, q, c) + (r % NC) * C, C), (1 - y) * 4 + q
-
-        def active(t):
-            return (t >= base) & (t < base + 4 * NC)
-
-        @pl.when(active(t - KEEP))
+            _, p, j, high = y_chunk(a, sent_at(t), short)
+            q = order(p, z)
+            return p * NC + j, rows(kept[a], place(1 - y, q, c) + j * C, high), (1 - y) * 4 + q
+
+        @pl.when(y_chunk(a, sent_at(t - KEEP), short)[0])
         def _():
             _, ref, idx = chunk(t - KEEP)
-            to_sibling(a, ref, idx, sib_send.at[2, a, (t - KEEP) % 4]).wait_send()
-
-        @pl.when(active(t))
+            to_sibling(a, ref, idx, y_sems(a, t - KEEP, short)[1]).wait_send()
+
+        @pl.when(y_chunk(a, sent_at(t), short)[0])
         def _():
             r, ref, idx = chunk(t)
-            pltpu.make_async_remote_copy(
-                ref, ref, y_send.at[a, 0], y_recv.at[a, r], **dev(1 - y, z, c)).wait_recv()
-            to_sibling(a, ref, idx, sib_send.at[2, a, t % 4]).start()
+            pltpu.make_async_remote_copy(ref, ref, y_send.at[a, 0], y_recv.at[a, r], **dev(1 - y, z, c)).wait_recv()
+            to_sibling(a, ref, idx, y_sems(a, t, short)[1]).start()
+
+    def pass_cut(d, t, arrive):
+        pos, nxt = step_of(d)
+        far = 1 if arrive else 0
+
+        def state(t):
+            ticks, last = ((CUT + 3, CUT + 6), (CUT + 6, CUT + 8, CUT + 10)) if arrive else ((CUT, CUT + 3), (CUT + 3, CUT + 4, CUT + 7))
+            at_last = pos == 2 + far
+            h = jnp.where(at_last, jnp.where(t == last[1], 1, jnp.where(t == last[2], 2, 0)), jnp.where(t == ticks[1], 1, 0))
+            on = jnp.where(at_last, (t == last[0]) | (t == last[1]) | (t == last[2]), (t == ticks[0]) | (t == ticks[1]))
+            on = on & (h + far <= pos) & (pos < 3 + far)
+            q = z_at(d, jnp.maximum(pos - far - h, 0))
+            ref = rows(gx, place(1 - y, q, c) + (R - CUT_ROWS), CUT_ROWS)
+            if arrive:
+                copy = to_sibling(1, ref, (1 - y) * 4 + q, cut_sib.at[d, h])
+            else:
+                copy = pltpu.make_async_remote_copy(ref, ref, cut_send.at[d, h], cut_recv.at[d, h], **dev(y, nxt, c))
+            return on, h, ref, copy
+
+        was, now = state(t - KEEP), state(t)
+
+        @pl.when(was[0])
+        def _():
+            was[3].wait_send()
+
+        @pl.when(now[0])
+        def _():
+            _, h, ref, copy = now
+            if arrive:
+                pltpu.make_async_remote_copy(ref, ref, cut_send.at[d, 0], cut_recv.at[d, h], **dev(y, z, 1 - c)).wait_recv()
+            copy.start()
 
     def own_to_sibling(a):
         return pltpu.make_async_remote_copy(
@@ -195,9 +238,12 @@
 
     def sum_state(d, t):
         pos, nxt = step_of(d)
-        on = (pos < 3) & (t >= 8 + 8 * pos) & (t < 32)
-        u = jnp.clip(t - 8 - 4 * pos, 0, 23)
-        k, j = u // NC, u % NC
+        first = jnp.where(pos == 0, SUMS - 1, SUMS + 6 * pos)
+        on = (pos < 3) & (t >= first) & (t < SUMS + 20 - 2 * pos - jnp.where(pos == 0, 1, 0))
+        u = jnp.clip(t - first, 0, 19)
+        early = (pos == 0) & (u == NC)
+        u = jnp.where((pos == 0) & (u > NC) & (u < 17), u - 1, u)
+        k, j = jnp.where(early, 5, pos + 1 + u // NC), jnp.where(early, 0, u % NC)
         to_pos = jnp.where(k < 3, k + 1, 6 - k)
         idx = jnp.where(k < 3, y, 1 - y) * 4 + z_at(d, to_pos)
         return on, pos, nxt, k, j, idx
@@ -251,62 +297,72 @@
 
             sum_send(d, t, nxt, k, j).start()
 
-    end, middle = 2, (z > 0) & (z < 3)
-
-    def end_loads(other, j, start):
-        idx = jnp.where(other, 1 - y, y) * 4 + z
-        if start:
-            @pl.when(j == 0)
-            def _():
-                wait_partial(idx)
-
-        for copy in (own_load(end, idx, j), sib_load(end, idx, j)):
-            copy.start() if start else copy.wait()
-        for d, there, slot in ((0, z > 0, 0), (1, z < 3, jnp.where(z > 0, 1, 0))):
-            pos, _ = step_of(d)
-            k = jnp.where(other, 6 - pos, pos - 1)
-
-            @pl.when(there)
-            def _(d=d, k=k, slot=slot):
-                if start:
-                    wait_in(d, k, j)
-                    in_load(end, slot, d, k, j).start()
-                else:
-                    in_load(end, slot, d, k, j).wait()
+    end = 2
 
     def end_state(t):
-        other = t >= OTHERS
-        return (t >= MINE) & (t < OTHERS + NC), other, jnp.clip(jnp.where(other, t - OTHERS, t - MINE), 0, NC - 1)
+        last = t >= OTHERS
+        kind = jnp.where(last, 3, jnp.clip((t - PARTS) // NC, 0, 2))
+        on = jnp.where(last, t < OTHERS + NC, (t >= PARTS) & (t < PARTS + 3 * NC))
+        on = on & ((kind != 1) | (z < 3)) & ((kind != 2) | (z > 0))
+        j = jnp.clip(jnp.where(last, t - OTHERS, (t - PARTS) % NC), 0, NC - 1)
+        idx = jnp.where(kind == 3, 1 - y, y) * 4 + z + jnp.where(kind == 1, 1, 0) - jnp.where(kind == 2, 1, 0)
+        idx = jnp.clip(idx, 0, 7)
+        left = (z > 0) & ((kind == 1) | (kind == 3))
+        right = (z < 3) & ((kind == 2) | (kind == 3))
+        back = 3 - z
+        arrived = (
+            (0, left, jnp.where(kind == 1, z, 6 - z), 0),
+            (1, right, jnp.where(kind == 2, back, 6 - back), jnp.where(left, 1, 0)),
+        )
+        return on, kind, j, idx, arrived
+
+    def end_loads(t, start):
+        on, _, j, idx, arrived = end_state(t)
+
+        @pl.when(on)
+        def _():
+            if start:
+                @pl.when(j == 0)
+                def _():
+                    wait_partial(idx)
+
+            for copy in (own_load(end, idx, j), sib_load(end, idx, j)):
+                copy.start() if start else copy.wait()
+            for d, there, k, slot in arrived:
+                @pl.when(there)
+                def _(d=d, k=jnp.clip(k, 0, 5), slot=slot):
+                    if start:
+                        wait_in(d, k, j)
+                        in_load(end, slot, d, k, j).start()
+                    else:
+                        in_load(end, slot, d, k, j).wait()
 
     def end_store(t, start):
-        on, other, j = end_state(t)
-        for mine in (True, False):
-            @pl.when(on & (other != mine))
-            def _(mine=mine):
-                src, dst = (own_b.at[end], mysum) if mine else (out_b.at[end, 0], ysum)
+        on, kind, j, _, _ = end_state(t)
+        for n, (src, dst) in enumerate((
+            (own_b.at[end], mysum), (out_b.at[end, 0], next_sum), (out_b.at[end, 0], back_sum), (out_b.at[end, 0], ysum),
+        )):
+            @pl.when(on & (kind == n))
+            def _(src=src, dst=dst):
                 copy = pltpu.make_async_copy(src, rows(dst, j * C, C), end_sem)
                 copy.start() if start else copy.wait()
 
     def last_loads(t):
         end_store(t - 1, False)
-        on, other, j = end_state(t)
-
-        @pl.when(on)
-        def _():
-            end_loads(other, j, True)
+        end_loads(t, True)
 
     def last_sum(t):
-        on, other, j = end_state(t)
-
-        @pl.when(on)
-        def _():
-            end_loads(other, j, False)
-
-        for mine in (True, False):
-            for n, where in ((2, middle), (1, jnp.logical_not(middle))):
-                @pl.when(on & (other != mine) & where)
-                def _(mine=mine, n=n):
-                    add(end, None if mine else 0, n)
+        end_loads(t, False)
+        on, kind, _, _, ((_, left, _, _), (_, right, _, _)) = end_state(t)
+
+        @pl.when(on & (kind == 0))
+        def _():
+            add(end, None, 0)
+
+        for n, where in ((0, jnp.logical_not(left | right)), (1, left != right), (2, left & right)):
+            @pl.when(on & (kind > 0) & where)
+            def _(n=n):
+                add(end, 0, n)
 
         end_store(t, True)
 
@@ -317,32 +373,49 @@
         def _(i):
             ref[pl.ds(pl.multiple_of(i * high, 8), high), :] = jnp.zeros((high, ref.shape[1]), F32)
 
-    def exchange(t, late):
-        for a in (0, 1):
+    def exchange(t, phase):
+        def holds(first, last):
+            return phase[0] <= last + KEEP and first < phase[1]
+
+        arrivals = ((LAG, 11 + LAG, LAG, 15 + LAG), (NC + LAG, 23 + LAG, Y_X + LAG, Y_X3 + 9 + LATE))
+        for a, (z_first, z_last, y_first, y_last) in enumerate(arrivals):
+            if holds(z_first, z_last):
+                for d in (0, 1):
+                    arrive_z(d, a, t)
+            if holds(y_first, y_last):
+                arrive_y(a, t)
+                if a:
+                    arrive_y(a, t, True)
+        for d in (0, 1):
+            if holds(CUT + 3, CUT + 10):
+                pass_cut(d, t, True)
+        for a, (z_first, z_last, y_first, y_last) in enumerate(((0, 11, 0, 15), (NC, 23, Y_X, Y_X3 + 9))):
+            if holds(y_first, y_last):
+                gather_y(a, t)
+                if a:
+                    gather_y(a, t, True)
+            if holds(z_first, z_last):
+                for d in (0, 1):
+                    gather_z(d, a, t)
+        for d in (0, 1):
+            if holds(CUT, CUT + 7):
+                pass_cut(d, t, False)
+        if holds(SUMS - 1, SUMS + 19):
             for d in (0, 1):
-                arrive_z(d, a, t)
-            arrive_y(a, t)
-        for a in (0, 1):
-            gather_y(a, t)
-            for d in (0, 1):
-                gather_z(d, a, t)
-        for d in (0, 1):
-            sum_loads(d, t)
-        if late:
-            last_loads(t)
-
-    def sums(t, late):
+                sum_loads(d, t)
+        last_loads(t)
+
+    def sums(t):
         for d in (0, 1):
             sum_add(d, t)
-        if late:
-            last_sum(t)
-
-    def spread(t, late, begin, end, step):
+        last_sum(t)
+
+    def spread(t, begin, end, step):
         @pl.loop(0, jnp.maximum(end - begin, 2))
         def _(n):
             @pl.when(n == 1)
             def _():
-                sums(t, late)
+                sums(t)
 
             @pl.when(begin + n < end)
             def _():
@@ -445,9 +518,9 @@
 
             @pl.loop(0, tiles)
             def _(tile):
-                @pl.when(tile == 1)
+                @pl.when((tile == 1) & (t != SUMS - 1))
                 def _():
-                    sums(t, False)
+                    sums(t)
 
                 slot = tile % 2
                 @pl.when(tile >= 2)
@@ -468,7 +541,9 @@
 
         @pl.loop(0, A_END)
         def _(t):
-            exchange(t, False)
+            @pl.when(t != SUMS - 1)
+            def _():
+                exchange(t, (0, A_END))
 
             @pl.when(t == 0)
             def _():
@@ -485,22 +560,27 @@
                 for a in (0, 1):
                     own_rows(1, a).wait()
 
-            n = jnp.maximum((t - 4) // 2, 0)
-
-            @pl.when((t == 2) | ((t >= 6) & (t % 2 == 0)))
+            n = jnp.clip((t - 3) // 2, 0, BLOCKS - 1)
+
+            @pl.when((t == 2) | ((t >= 5) & (t % 2 == 1)))
             def _():
                 idx = block_of(n)
                 wait_sibling(0, idx)
                 load = pltpu.make_async_copy(rows(gdy, idx * B, B), dy_v, dy_sem)
                 load.start()
 
-                sums(t, False)
+                sums(t)
                 load.wait()
                 gradients(n)
 
-            @pl.when((t == 3) | ((t >= 7) & (t % 2 == 1)))
+            @pl.when((t == 3) | ((t >= 6) & (t % 2 == 0)))
             def _():
                 dx_terms(t, n)
+
+                @pl.when(t == SUMS - 1)
+                def _():
+                    exchange(t, (0, A_END))
+                    sums(t)
 
     pl.run_scoped(
         first,
@@ -556,14 +636,14 @@
 
         @pl.loop(A_END, B_END)
         def _(t):
-            exchange(t, False)
+            exchange(t, (A_END, B_END))
 
             @pl.when(t == A_END)
             def _():
                 hidden.wait()
 
             begin = (t - A_END) * per_tick
-            spread(t, False, begin, jnp.minimum(begin + per_tick, steps), step)
+            spread(t, begin, jnp.minimum(begin + per_tick, steps), step)
 
         result(wide - 1).wait()
 
@@ -604,7 +684,7 @@
 
         @pl.loop(B_END, N_END)
         def _(t):
-            exchange(t, True)
+            exchange(t, (B_END, N_END))
 
             @pl.when(t == B_END)
             def _():
@@ -615,7 +695,7 @@
                     copy.wait()
 
             begin = (t - B_END) * per_tick
-            spread(t, True, begin, jnp.minimum(begin + per_tick, steps), step)
+            spread(t, begin, jnp.minimum(begin + per_tick, steps), step)
 
         for i in (steps - 2, steps - 1):
             result(i).wait()
@@ -626,11 +706,16 @@
         pltpu.SemaphoreType.DMA((2,)), pltpu.SemaphoreType.DMA((2,)), pltpu.SemaphoreType.DMA((2,)),
     )
 
-    @pl.loop(N_END, T_END + KEEP)
+    @pl.loop(N_END, T_END)
     def _(t):
-        exchange(t, True)
-        sums(t, True)
-
+        exchange(t, (N_END, T_END))
+        sums(t)
+
+    for t in range(T_END, T_END + KEEP):
+        arrive_y(1, t)
+        arrive_y(1, t, True)
+        for d in (0, 1):
+            pass_cut(d, t, True)
     for q in range(4):
         wait_sibling(1, (1 - y) * 4 + q)
     for a in (0, 1):
@@ -647,8 +732,8 @@
     def tiles(i):
         at = pl.multiple_of(i * TM, 128)
         return [
-            pltpu.make_async_copy(gx.at[half, pl.ds(at, TM)], x_v.at[i % 2], x_sem.at[i % 2]),
-            pltpu.make_async_copy(part.at[pl.ds(at, TM)], p_v.at[i % 2], p_sem.at[i % 2]),
+            pltpu.make_async_copy(gx.at[half, pl.ds(at, TM)], x_v.at[i % 3], x_sem.at[i % 3]),
+            pltpu.make_async_copy(part.at[pl.ds(at, TM)], p_v.at[i % 3], p_sem.at[i % 3]),
         ]
 
     def results(i):
@@ -661,36 +746,38 @@
             return pltpu.make_async_copy(down.at[at], down_v.at[at], c_sem.at[0, i])
         return pltpu.make_async_copy(down_v.at[at], dwd.at[at], c_sem.at[1, i])
 
-    for copy in grads + tiles(0):
+    for copy in grads + tiles(0) + tiles(1):
         copy.start()
     for copy in grads:
         copy.wait()
-    for i in range(pieces):
-        piece(0, i).start()
 
     @pl.loop(0, steps)
     def _(i):
         for copy in tiles(i):
             copy.wait()
 
-        @pl.when(i + 1 < steps)
-        def _():
-            for copy in tiles(i + 1):
+        @pl.when(i + 2 < steps)
+        def _():
+            for copy in tiles(i + 2):
                 copy.start()
 
         @pl.when(i < pieces)
         def _():
-            piece(0, i).wait()
-            piece(1, i).start()
+            piece(0, i).start()
+
+        @pl.when((i >= 2) & (i < pieces + 2))
+        def _():
+            piece(0, i - 2).wait()
+            piece(1, i - 2).start()
 
         @pl.when(i >= 2)
         def _():
             for copy in results(i - 2):
                 copy.wait()
 
-        p_v[i % 2] += lax.dot_general(x_v[i % 2], d_v[...], (((0,), (0,)), ((), ())), preferred_element_type=F32)
+        total = p_v[i % 3] + lax.dot_general(x_v[i % 3], d_v[...], (((0,), (0,)), ((), ())), preferred_element_type=F32)
         for n in (0, 1):
-            out_v[i % 2, n] = p_v[i % 2, :, pl.ds(n * F, F)].astype(BF16)
+            out_v[i % 2, n] = total[:, n * F : (n + 1) * F].astype(BF16)
         for copy in results(i):
             copy.start()
 
@@ -707,46 +794,51 @@
     hbm = pl.BlockSpec(memory_space=pl.ANY)
     shape, vmem, dma = jax.ShapeDtypeStruct, pltpu.VMEM, pltpu.SemaphoreType.DMA
     outs = (
-        shape((R, D), BF16), shape((R, D), F32), shape((F, D), BF16), shape((D, 2 * F), F32),
+        shape((R, D), BF16), shape((R, D), F32), shape((R, D), BF16), shape((R, D), BF16), shape((F, D), BF16), shape((D, 2 * F), F32),
         shape((T, D), BF16), shape((T, D), BF16), shape((T // 2, D), F32), shape((T // 2, D), BF16),
         shape((2, 6 * R, D), BF16), shape((T, F), BF16), shape((T, F), BF16), shape((T, F), BF16),
     )
     product = 2 * T * D * F
-    ysum, mysum, down, part, gx, _, _, _, _, dgs, dus, _ = pl.pallas_call(
+    ysum, mysum, next_sum, back_sum, down, part, gx, _, _, _, _, dgs, dus, _ = pl.pallas_call(
         functools.partial(kernel, dims),
         out_shape=outs,
         in_specs=[hbm] * 7,
         out_specs=[hbm] * len(outs),
         scratch_shapes=[
             vmem((3, C, D), F32), vmem((3, C, D), BF16), vmem((3, 2, C, D), BF16), vmem((3, 3, C, D), BF16),
-            dma((2, 2, 4)), dma((2, 2, 12)), dma((2, 4)), dma((2, 16)), dma((3, 2, 4)), dma((2, 8)), dma((2,)),
+            dma((2, 2, 4)), dma((2, 2, 12)), dma((2, 4)), dma((2, 16)), dma((2,)), dma((3, 2, 4)), dma((2, 8)), dma((2,)), dma((2,)),
+            dma((2, 3)), dma((2, 3)), dma((2, 3)),
             dma((2, 3)), dma((2, 24)), dma((BLOCKS,)), dma((3, 4)), dma,
         ],
         compiler_params=pltpu.CompilerParams(collective_id=0, has_side_effects=True, vmem_limit_bytes=67043328),
         cost_estimate=pl.CostEstimate(flops=5 * product, bytes_accessed=10 * T * D, transcendentals=0),
         name="mlp_backward",
     )(x, dy, gate, up, wg, wu, wd)
-    across = lax.ppermute(ysum, "tp", [(i, (i + 8) % 16) for i in range(16)])
+    sums = [
+        lax.ppermute(ysum, "tp", [(i, (i + 8) % 16) for i in range(16)]),
+        lax.ppermute(next_sum, "tp", [(i, i + 2) for i in range(16) if i // 2 % 4 < 3]),
+        lax.ppermute(back_sum, "tp", [(i, i - 2) for i in range(16) if i // 2 % 4 > 0]),
+    ]
     weights = pl.pallas_call(
         functools.partial(finish_kernel, dims),
         out_shape=(shape((D, F), BF16), shape((D, F), BF16), shape((F, D), BF16)),
         in_specs=[hbm] * 5,
         out_specs=[hbm] * 3,
         scratch_shapes=[
-            vmem((T // 2, 2 * F), BF16), vmem((2, T // 2, TM), BF16), vmem((2, TM, 2 * F), F32), vmem((2, 2, TM, F), BF16),
-            vmem((F, D), BF16), dma((2,)), dma((2,)), dma((2,)), dma((2, 2)), dma((2, 8)),
+            vmem((T // 2, 2 * F), BF16), vmem((3, T // 2, TM), BF16), vmem((3, TM, 2 * F), F32), vmem((2, 2, TM, F), BF16),
+            vmem((F, D), BF16), dma((2,)), dma((3,)), dma((3,)), dma((2, 2)), dma((2, 8)),
         ],
         compiler_params=pltpu.CompilerParams(vmem_limit_bytes=67043328),
         cost_estimate=pl.CostEstimate(flops=product, bytes_accessed=6 * T * D, transcendentals=0),
         name="finish",
     )(part, gx, dgs, dus, down)
-    return ((mysum + across.astype(F32)).astype(BF16), *weights)
+    return (sum((a.astype(F32) for a in sums), mysum).astype(BF16), *weights)
 
 
 def solution(mesh):
     def step(x, dy, gate, up, wg, wu, wd):
         (rows, depth), wide = x.shape, wg.shape[1]
-        dims = (rows, depth, wide, 512, 1024, 256, 1280, 512, 1024)
+        dims = (rows, depth, wide, 512, 1024, 256, 1280, 512, 1024, 32)
         return fused(dims, x, dy, gate, up, wg, wu, wd)
 
     tokens, columns = P(("dp", "tp"), None), P("dp", "tp")

time: 466 us -> 455 us (0.976)
  Pallas kernels: 457 us -> 432 us
  starting transfers between devices: 1.21 us -> 11.6 us
    pallas_call x1, Pallas kernels: 404 us -> 384 us  [fused(): pl.pallas_call(functools.partial(kernel, dims), out_shape=outs, in_specs=...]
    ppermute x1 -> x3, starting transfers between devices: 1.21 us -> 11.6 us  [the longest x1 8.58 us: fused(): lax.ppermute(next_sum, 'tp', [(i, i + 2) for i in range(16) if i // 2 % 4...]
    pallas_call x1, Pallas kernels: 53.7 us -> 48.2 us  [fused(): pl.pallas_call(functools.partial(finish_kernel, dims), out_shape=(shape((...]
  transfers between devices with their start and end apart: 1 -> 3, of which waited for: 0 -> 1; matrix products, arithmetic and copies ran while one was open for 0% -> 0% of each run, Pallas kernels for 12% -> 11%
where the time goes in v3:
time: 455 us
  Pallas kernels  432 us (95%)
  starting transfers between devices  11.6 us (3%)
  other arithmetic  7.01 us (2%)
    pallas_call x1, Pallas kernels, fused(): pl.pallas_call(functools.partial(kernel, dims), out_shape=outs, in_specs=...  384 us
    pallas_call x1, Pallas kernels, fused(): pl.pallas_call(functools.partial(finish_kernel, dims), out_shape=(shape((...  48.2 us
  transfers between devices with their start and end apart: 3, of which 1 were waited for; matrix products, arithmetic and copies ran while one was open for 0% of the time, Pallas kernels for 11%

profile of v3, /device:TPU:0, one launch (start us, length us, event | category | flops | bytes accessed | tf_op | source)
XLA Modules:
  0.0 454.7 jit_solution(3580441133193538867)
XLA Ops:
  0.6 383.5 %mlp_backward.1 = (bf16[224,5120]{1,0:T(8,128)(2,1)}, f32[224,5120]{1,0:T(8,128)}, bf16[224,5120]{1,0:T(8,128)(2,1)}, bf16[224,5120]{1,0:T(8,128)(2,1)}, bf16[10...) custom-call(bf16[224,5120]{1,0:T(8,128)(2,1)} %x.1, ...), custom_call_target="tpu_custom_call" | custom-call | flops 187904819200 | bytes 183500800 | tf_op jit(solution)/shard_map/mlp_backward/pallas_call | solution.py:802
  384.2 1.6 collective-permute-start
  385.7 8.6 %collective-permute-start.1 = (bf16[224,5120]{1,0:T(8,128)(2,1)}, bf16[224,5120]{1,0:T(8,128)(2,1)}, u32[]{:S(2)}, u32[]{:S(2)}) collective-permute-start(bf16[224,5120]{1,0:T(8,128)(2,1)} %get-tuple-element.18), channel_id=1, source_target_pairs={{0,2},{1,3},{2,4},{3,5},{4,6},{5,7},{8,10},{9,11},{10,12},{11,13},... | collective-permute-start | bytes 6881288 | tf_op jit(solution)/shard_map/ppermute | solution.py:819
  394.3 1.5 collective-permute-start.2
  395.8 48.2 %finish.1 = (bf16[5120,1024]{1,0:T(8,128)(2,1)}, bf16[5120,1024]{1,0:T(8,128)(2,1)}, bf16[1024,5120]{1,0:T(8,128)(2,1)}) custom-call(f32[5120,2048]{1,0:T(8,128)} %get-tuple-element.20.part, bf16[3584,5120]{1,0:T(8,128)(2,1)} %get-tuple-element.21.gx, bf16[3584,1024]{1,0:T(8,128)(2,1)} %get-tuple-element.22.dgs, bf16[3584,1024]{1,0:T(8,128)(2,1)} %get-tuple-element.23.dus, ...), custom_call_target="tpu_custom_call" | custom-call | flops 37580963840 | bytes 110100480 | tf_op jit(solution)/shard_map/finish/pallas_call | solution.py:822
  444.0 0.0 collective-permute-done
  444.0 0.0 collective-permute-done.1
  444.0 3.7 collective-permute-done.2
  447.7 7.0 %add_convert_fusion = bf16[224,5120]{1,0:T(8,128)(2,1)} fusion(bf16[224,5120]{1,0:T(8,128)(2,1)} %collective-permute-done.2, bf16[224,5120]{1,0:T(8,128)(2,1)} %collective-permute-done.1, f32[224,5120]{1,0:T(8,128)} %get-tuple-element.16, bf16[224,5120]{1,0:T(8,128)(2,1)} %collective-permute-done), kind=kLoop, calls=%fused_computation | loop fusion | flops 8028160 | bytes 13762560 | tf_op jit(solution)/shard_map/convert_element_type | solution.py:835
Async XLA Ops:
  384.2 59.8 %collective-permute-start = (bf16[224,5120]{1,0:T(8,128)(2,1)}, bf16[224,5120]{1,0:T(8,128)(2,1)}, u32[]{:S(2)}, u32[]{:S(2)}) collective-permute-start(bf16[224,5120]{1,0:T(8,128)(2,1)} %get-tuple-element.17), channel_id=1, source_target_pairs={{0,8},{1,9},{2,10},{3,11},{4,12},{5,13},{6,14},{7,15},{8,0},{9,1},... | collective-permute-start | bytes 6881288 | tf_op jit(solution)/shard_map/ppermute | solution.py:818
  385.7 58.2 %collective-permute-start.1 = (bf16[224,5120]{1,0:T(8,128)(2,1)}, bf16[224,5120]{1,0:T(8,128)(2,1)}, u32[]{:S(2)}, u32[]{:S(2)}) collective-permute-start(bf16[224,5120]{1,0:T(8,128)(2,1)} %get-tuple-element.18), channel_id=1, source_target_pairs={{0,2},{1,3},{2,4},{3,5},{4,6},{5,7},{8,10},{9,11},{10,12},{11,13},... | collective-permute-start | bytes 6881288 | tf_op jit(solution)/shard_map/ppermute | solution.py:819
  394.3 53.4 %collective-permute-start.2 = (bf16[224,5120]{1,0:T(8,128)(2,1)}, bf16[224,5120]{1,0:T(8,128)(2,1)}, u32[]{:S(2)}, u32[]{:S(2)}) collective-permute-start(bf16[224,5120]{1,0:T(8,128)(2,1)} %get-tuple-element.19), channel_id=1, source_target_pairs={{2,0},{3,1},{4,2},{5,3},{6,4},{7,5},{10,8},{11,9},{12,10},{13,11},... | collective-permute-start | bytes 6881288 | tf_op jit(solution)/shard_map/ppermute | solution.py:820

commit v4 on v3

--- a/solution.py
+++ b/solution.py
@@ -21,8 +21,21 @@
 A_END, B_END, N_END, T_END = 19, 25, 29, 33
 
 
+BOTH, PAIR = (0, 1), 2
+LAST = 3
+LANES, ROWS = (((1,), (1,)), ((), ())), (((0,), (0,)), ((), ()))
+
+
+def lanes(start, n):
+    return pl.ds(pl.multiple_of(start, 128), n)
+
+
+def subs(start, n):
+    return pl.ds(pl.multiple_of(start, 8), n)
+
+
 def order(p, z):
-    near = jnp.where(z < 2, z, 3 - z)
+    near = jnp.where(z < 2, z, LAST - z)
     q = jnp.where((near == 1) & (p < 2), 1 - p, p)
     return jnp.where(z < 2, q, 3 - q)
 
@@ -30,7 +43,7 @@
 def kernel(
     dims,
     x, dy, gate, up, wg, wu, wd,
-    ysum, mysum, next_sum, back_sum, dwd, part, gx, gdy, own, sib, ins, dgs, dus, hids,
+    ysum, mysum, pair_sum, inner_sum, dwd, part, gx, gdy, own, sib, ins, dgs, dus, hids,
     own_b, sib_b, in_b, out_b,
     z_send, z_recv, y_send, y_recv, short_send, sib_send, sib_recv, sib_short, own_send, cut_send, cut_recv, cut_sib,
     rs_send, rs_recv, dxs_recv, load_sem, end_sem,
@@ -39,22 +52,23 @@
     C, B, T = R // NC, 2 * R, 2 * R * BLOCKS
     dp, tp = lax.axis_index("dp"), lax.axis_index("tp")
     y, z, c = tp // 8, (tp // 2) % 4, tp % 2
+    opp, mate = 1 - y, 1 - c
     sent, kept = (dy, x), (gdy, gx)
 
     def dev(yy, zz, cc):
         return dict(device_id=(dp, yy * 8 + zz * 2 + cc), device_id_type=MESH)
 
     def rows(ref, start, n):
-        return ref.at[pl.ds(pl.multiple_of(start, 8), n)]
+        return ref.at[subs(start, n)]
 
     def place(yy, zz, cc):
         return ((yy * 4 + zz) * 2 + cc) * R
 
     def step_of(d):
-        return (z, jnp.minimum(z + 1, 3)) if d == 0 else (3 - z, jnp.maximum(z - 1, 0))
+        return (z, jnp.minimum(z + 1, LAST)) if d == 0 else (LAST - z, jnp.maximum(z - 1, 0))
 
     def z_at(d, pos):
-        return pos if d == 0 else 3 - pos
+        return pos if d == 0 else LAST - pos
 
     def gather_z(d, a, t):
         pos, nxt = step_of(d)
@@ -69,7 +83,7 @@
                 src, there, z_send.at[d, a, t % 4], z_recv.at[d, a, s], **dev(y, nxt, c))
 
         def active(t):
-            return (pos < 3) & (t >= base) & (t < base + NC * (pos + 1))
+            return (pos < LAST) & (t >= base) & (t < base + NC * (pos + 1))
 
         @pl.when(active(t - KEEP))
         def _():
@@ -84,7 +98,7 @@
             copy(t).start()
 
     def to_sibling(a, ref_rows, idx, sem):
-        return pltpu.make_async_remote_copy(ref_rows, ref_rows, sem, sib_recv.at[a, idx], **dev(y, z, 1 - c))
+        return pltpu.make_async_remote_copy(ref_rows, ref_rows, sem, sib_recv.at[a, idx], **dev(y, z, mate))
 
     def arrive_z(d, a, t):
         pos, _ = step_of(d)
@@ -107,7 +121,7 @@
         def _():
             r, ref, idx = chunk(t)
             pltpu.make_async_remote_copy(
-                ref, ref, z_send.at[d, a, 0], z_recv.at[d, a, r], **dev(y, z, 1 - c)).wait_recv()
+                ref, ref, z_send.at[d, a, 0], z_recv.at[d, a, r], **dev(y, z, mate)).wait_recv()
             to_sibling(a, ref, idx, sib_send.at[d, a, t % 4]).start()
 
     def y_chunk(a, t, short):
@@ -128,7 +142,7 @@
             _, p, j, high = y_chunk(a, t, short)
             there = rows(kept[a], place(y, order(p, z), c) + j * C, high)
             src = rows(sent[a], j * C, high) if own_rows else there
-            return pltpu.make_async_remote_copy(src, there, y_sems(a, t, short)[0], y_recv.at[a, p * NC + j], **dev(1 - y, z, c))
+            return pltpu.make_async_remote_copy(src, there, y_sems(a, t, short)[0], y_recv.at[a, p * NC + j], **dev(opp, z, c))
 
         was, (on, p, _, _) = y_chunk(a, t - KEEP, short)[0], y_chunk(a, t, short)
 
@@ -154,7 +168,7 @@
         def chunk(t):
             _, p, j, high = y_chunk(a, sent_at(t), short)
             q = order(p, z)
-            return p * NC + j, rows(kept[a], place(1 - y, q, c) + j * C, high), (1 - y) * 4 + q
+            return p * NC + j, rows(kept[a], place(opp, q, c) + j * C, high), opp * 4 + q
 
         @pl.when(y_chunk(a, sent_at(t - KEEP), short)[0])
         def _():
@@ -164,7 +178,7 @@
         @pl.when(y_chunk(a, sent_at(t), short)[0])
         def _():
             r, ref, idx = chunk(t)
-            pltpu.make_async_remote_copy(ref, ref, y_send.at[a, 0], y_recv.at[a, r], **dev(1 - y, z, c)).wait_recv()
+            pltpu.make_async_remote_copy(ref, ref, y_send.at[a, 0], y_recv.at[a, r], **dev(opp, z, c)).wait_recv()
             to_sibling(a, ref, idx, y_sems(a, t, short)[1]).start()
 
     def pass_cut(d, t, arrive):
@@ -176,11 +190,11 @@
             at_last = pos == 2 + far
             h = jnp.where(at_last, jnp.where(t == last[1], 1, jnp.where(t == last[2], 2, 0)), jnp.where(t == ticks[1], 1, 0))
             on = jnp.where(at_last, (t == last[0]) | (t == last[1]) | (t == last[2]), (t == ticks[0]) | (t == ticks[1]))
-            on = on & (h + far <= pos) & (pos < 3 + far)
+            on = on & (h + far <= pos) & (pos < LAST + far)
             q = z_at(d, jnp.maximum(pos - far - h, 0))
-            ref = rows(gx, place(1 - y, q, c) + (R - CUT_ROWS), CUT_ROWS)
+            ref = rows(gx, place(opp, q, c) + (R - CUT_ROWS), CUT_ROWS)
             if arrive:
-                copy = to_sibling(1, ref, (1 - y) * 4 + q, cut_sib.at[d, h])
+                copy = to_sibling(1, ref, opp * 4 + q, cut_sib.at[d, h])
             else:
                 copy = pltpu.make_async_remote_copy(ref, ref, cut_send.at[d, h], cut_recv.at[d, h], **dev(y, nxt, c))
             return on, h, ref, copy
@@ -195,20 +209,20 @@
         def _():
             _, h, ref, copy = now
             if arrive:
-                pltpu.make_async_remote_copy(ref, ref, cut_send.at[d, 0], cut_recv.at[d, h], **dev(y, z, 1 - c)).wait_recv()
+                pltpu.make_async_remote_copy(ref, ref, cut_send.at[d, 0], cut_recv.at[d, h], **dev(y, z, mate)).wait_recv()
             copy.start()
 
     def own_to_sibling(a):
         return pltpu.make_async_remote_copy(
-            sent[a], rows(kept[a], place(y, z, c), R), own_send.at[a], sib_recv.at[a, y * 4 + z], **dev(y, z, 1 - c))
+            sent[a], rows(kept[a], place(y, z, c), R), own_send.at[a], sib_recv.at[a, y * 4 + z], **dev(y, z, mate))
 
     def wait_sibling(a, idx):
         ref = rows(kept[a], idx * B, R)
-        pltpu.make_async_remote_copy(ref, ref, own_send.at[a], sib_recv.at[a, idx], **dev(y, z, 1 - c)).wait_recv()
+        pltpu.make_async_remote_copy(ref, ref, own_send.at[a], sib_recv.at[a, idx], **dev(y, z, mate)).wait_recv()
 
     def wait_partial(idx):
         ref = rows(sib, idx * R, R)
-        pltpu.make_async_remote_copy(ref, ref, own_send.at[0], dxs_recv.at[idx], **dev(y, z, 1 - c)).wait_recv()
+        pltpu.make_async_remote_copy(ref, ref, own_send.at[0], dxs_recv.at[idx], **dev(y, z, mate)).wait_recv()
 
     def own_load(b, idx, j):
         return pltpu.make_async_copy(rows(own, idx * R + j * C, C), own_b.at[b], load_sem.at[b, 0])
@@ -222,12 +236,12 @@
     def wait_in(d, k, j):
         ref = rows(ins.at[d], k * R + j * C, C)
         pltpu.make_async_remote_copy(
-            ref, ref, rs_send.at[d, 0], rs_recv.at[d, k * NC + j], **dev(y, z, 1 - c)).wait_recv()
+            ref, ref, rs_send.at[d, 0], rs_recv.at[d, k * NC + j], **dev(y, z, mate)).wait_recv()
 
     def add(b, slot, n):
         @pl.loop(0, D // TV)
         def _(i):
-            cols = pl.ds(pl.multiple_of(i * TV, 128), TV)
+            cols = lanes(i * TV, TV)
             total = own_b[b, :, cols] + sib_b[b, :, cols].astype(F32)
             for m in range(n):
                 total = total + in_b[b, m, :, cols].astype(F32)
@@ -239,13 +253,13 @@
     def sum_state(d, t):
         pos, nxt = step_of(d)
         first = jnp.where(pos == 0, SUMS - 1, SUMS + 6 * pos)
-        on = (pos < 3) & (t >= first) & (t < SUMS + 20 - 2 * pos - jnp.where(pos == 0, 1, 0))
+        on = (pos < LAST) & (t >= first) & (t < SUMS + 20 - 2 * pos - jnp.where(pos == 0, 1, 0))
         u = jnp.clip(t - first, 0, 19)
         early = (pos == 0) & (u == NC)
         u = jnp.where((pos == 0) & (u > NC) & (u < 17), u - 1, u)
         k, j = jnp.where(early, 5, pos + 1 + u // NC), jnp.where(early, 0, u % NC)
         to_pos = jnp.where(k < 3, k + 1, 6 - k)
-        idx = jnp.where(k < 3, y, 1 - y) * 4 + z_at(d, to_pos)
+        idx = jnp.where(k < 3, y, opp) * 4 + z_at(d, to_pos)
         return on, pos, nxt, k, j, idx
 
     def sum_send(d, t, nxt, k, j):
@@ -303,13 +317,13 @@
         last = t >= OTHERS
         kind = jnp.where(last, 3, jnp.clip((t - PARTS) // NC, 0, 2))
         on = jnp.where(last, t < OTHERS + NC, (t >= PARTS) & (t < PARTS + 3 * NC))
-        on = on & ((kind != 1) | (z < 3)) & ((kind != 2) | (z > 0))
+        on = on & ((kind != 1) | (z < LAST)) & ((kind != 2) | (z > 0))
         j = jnp.clip(jnp.where(last, t - OTHERS, (t - PARTS) % NC), 0, NC - 1)
-        idx = jnp.where(kind == 3, 1 - y, y) * 4 + z + jnp.where(kind == 1, 1, 0) - jnp.where(kind == 2, 1, 0)
+        idx = jnp.where(kind == 3, opp, y) * 4 + z + jnp.where(kind == 1, 1, 0) - jnp.where(kind == 2, 1, 0)
         idx = jnp.clip(idx, 0, 7)
         left = (z > 0) & ((kind == 1) | (kind == 3))
-        right = (z < 3) & ((kind == 2) | (kind == 3))
-        back = 3 - z
+        right = (z < LAST) & ((kind == 2) | (kind == 3))
+        back = LAST - z
         arrived = (
             (0, left, jnp.where(kind == 1, z, 6 - z), 0),
             (1, right, jnp.where(kind == 2, back, 6 - back), jnp.where(left, 1, 0)),
@@ -339,10 +353,15 @@
 
     def end_store(t, start):
         on, kind, j, _, _ = end_state(t)
-        for n, (src, dst) in enumerate((
-            (own_b.at[end], mysum), (out_b.at[end, 0], next_sum), (out_b.at[end, 0], back_sum), (out_b.at[end, 0], ysum),
-        )):
-            @pl.when(on & (kind == n))
+        along = (kind == 1) | (kind == 2)
+        paired = (kind == 1) == (z % 2 == 0)
+        for where, src, dst in (
+            (kind == 0, own_b.at[end], mysum),
+            (along & paired, out_b.at[end, 0], pair_sum),
+            (along & jnp.logical_not(paired), out_b.at[end, 0], inner_sum),
+            (kind == 3, out_b.at[end, 0], ysum),
+        ):
+            @pl.when(on & where)
             def _(src=src, dst=dst):
                 copy = pltpu.make_async_copy(src, rows(dst, j * C, C), end_sem)
                 copy.start() if start else copy.wait()
@@ -371,7 +390,7 @@
 
         @pl.loop(0, ref.shape[0] // high)
         def _(i):
-            ref[pl.ds(pl.multiple_of(i * high, 8), high), :] = jnp.zeros((high, ref.shape[1]), F32)
+            ref[subs(i * high, high), :] = jnp.zeros((high, ref.shape[1]), F32)
 
     def exchange(t, phase):
         def holds(first, last):
@@ -380,13 +399,13 @@
         arrivals = ((LAG, 11 + LAG, LAG, 15 + LAG), (NC + LAG, 23 + LAG, Y_X + LAG, Y_X3 + 9 + LATE))
         for a, (z_first, z_last, y_first, y_last) in enumerate(arrivals):
             if holds(z_first, z_last):
-                for d in (0, 1):
+                for d in BOTH:
                     arrive_z(d, a, t)
             if holds(y_first, y_last):
                 arrive_y(a, t)
                 if a:
                     arrive_y(a, t, True)
-        for d in (0, 1):
+        for d in BOTH:
             if holds(CUT + 3, CUT + 10):
                 pass_cut(d, t, True)
         for a, (z_first, z_last, y_first, y_last) in enumerate(((0, 11, 0, 15), (NC, 23, Y_X, Y_X3 + 9))):
@@ -395,18 +414,18 @@
                 if a:
                     gather_y(a, t, True)
             if holds(z_first, z_last):
-                for d in (0, 1):
+                for d in BOTH:
                     gather_z(d, a, t)
-        for d in (0, 1):
+        for d in BOTH:
             if holds(CUT, CUT + 7):
                 pass_cut(d, t, False)
         if holds(SUMS - 1, SUMS + 19):
-            for d in (0, 1):
+            for d in BOTH:
                 sum_loads(d, t)
         last_loads(t)
 
     def sums(t):
-        for d in (0, 1):
+        for d in BOTH:
             sum_add(d, t)
         last_sum(t)
 
@@ -422,10 +441,10 @@
                 step(begin + n)
 
     barrier = pltpu.get_barrier_semaphore()
-    pl.semaphore_signal(barrier, 1, **dev(y, z, 1 - c))
-    pl.semaphore_signal(barrier, 1, **dev(1 - y, z, c))
-
-    @pl.when(z < 3)
+    pl.semaphore_signal(barrier, 1, **dev(y, z, mate))
+    pl.semaphore_signal(barrier, 1, **dev(opp, z, c))
+
+    @pl.when(z < LAST)
     def _():
         pl.semaphore_signal(barrier, 1, **dev(y, z + 1, c))
 
@@ -433,8 +452,8 @@
     def _():
         pl.semaphore_signal(barrier, 1, **dev(y, z - 1, c))
 
-    pl.semaphore_wait(barrier, jnp.where((z > 0) & (z < 3), 4, 3))
-    for a in (0, 1):
+    pl.semaphore_wait(barrier, jnp.where((z > 0) & (z < LAST), 4, 3))
+    for a in BOTH:
         own_to_sibling(a).start()
 
     def first(wd_v, wg_v, wu_v, dy_v, gate_v, up_v, dg_v, du_v, hid_v, stf, stb, w_sem, b_sem, dy_sem, g_sem, st_sem, dx_sem, dxs_send):
@@ -443,7 +462,7 @@
         def block_of(n):
             other = (n == 2) | (n == 4) | (n >= 6)
             p = jnp.where(other, jnp.where(n == 7, 3, n // 2 - 1), jnp.where(n < 2, n, (n + 1) // 2))
-            return jnp.where(other, 1 - y, y) * 4 + order(p, z)
+            return jnp.where(other, opp, y) * 4 + order(p, z)
 
         def gate_up(n):
             at = block_of(n) * B
@@ -461,12 +480,12 @@
             return pltpu.make_async_copy(part, rows(kept[a], place(y, z, c), R), b_sem.at[a])
 
         def terms(n, tile, slot):
-            at, cols = block_of(n) * R, pl.ds(pl.multiple_of(tile * TN, 128), TN)
+            at, cols = block_of(n) * R, lanes(tile * TN, TN)
             mine = pltpu.make_async_copy(
-                stf.at[slot, pl.ds(pl.multiple_of(c * R, 8), R)], own.at[pl.ds(pl.multiple_of(at, 8), R), cols], dx_sem.at[slot])
+                stf.at[slot, subs(c * R, R)], own.at[subs(at, R), cols], dx_sem.at[slot])
             theirs = pltpu.make_async_remote_copy(
-                stb.at[slot, pl.ds(pl.multiple_of((1 - c) * R, 8), R)], sib.at[pl.ds(pl.multiple_of(at, 8), R), cols],
-                dxs_send.at[slot], dxs_recv.at[block_of(n)], **dev(y, z, 1 - c))
+                stb.at[slot, subs(mate * R, R)], sib.at[subs(at, R), cols],
+                dxs_send.at[slot], dxs_recv.at[block_of(n)], **dev(y, z, mate))
             return mine, theirs
 
         def wait_terms(n, tile, slot):
@@ -480,7 +499,7 @@
             for copy in kept_grads(n):
                 copy.wait()
             for tile in (tiles - 2, tiles - 1):
-                wait_terms(n, tile, tile % 2)
+                wait_terms(n, tile, tile % PAIR)
 
         def gradients(n):
             @pl.when(n == 0)
@@ -492,9 +511,9 @@
 
             @pl.loop(0, F // TF)
             def _(i):
-                cols = pl.ds(pl.multiple_of(i * TF, 128), TF)
+                cols = lanes(i * TF, TF)
                 dh = lax.dot_general(
-                    dy_v[...], wd_v[pl.ds(pl.multiple_of(i * TF, 128), TF), :], (((1,), (1,)), ((), ())), preferred_element_type=F32)
+                    dy_v[...], wd_v[lanes(i * TF, TF), :], LANES, preferred_element_type=F32)
                 g, u = gate_v[:, cols].astype(F32), up_v[:, cols].astype(F32)
                 s = jax.nn.sigmoid(g)
                 silu = g * s
@@ -522,13 +541,13 @@
                 def _():
                     sums(t)
 
-                slot = tile % 2
+                slot = tile % PAIR
                 @pl.when(tile >= 2)
                 def _():
                     wait_terms(n, tile - 2, slot)
 
-                at = pl.ds(pl.multiple_of(tile * TN, 128), TN)
-                nt = (((1,), (1,)), ((), ()))
+                at = lanes(tile * TN, TN)
+                nt = LANES
                 total = lax.dot_general(dg_v[...], wg_v[at, :], nt, preferred_element_type=F32)
                 total = total + lax.dot_general(du_v[...], wu_v[at, :], nt, preferred_element_type=F32)
                 stf[slot] = total
@@ -547,17 +566,17 @@
 
             @pl.when(t == 0)
             def _():
-                for a in (0, 1):
+                for a in BOTH:
                     own_rows(0, a).start()
                 for copy in gate_up(0) + weights:
                     copy.start()
 
             @pl.when(t == 1)
             def _():
-                for a in (0, 1):
+                for a in BOTH:
                     own_rows(0, a).wait()
                     own_rows(1, a).start()
-                for a in (0, 1):
+                for a in BOTH:
                     own_rows(1, a).wait()
 
             n = jnp.clip((t - 3) // 2, 0, BLOCKS - 1)
@@ -587,9 +606,9 @@
         pltpu.VMEM((F, D), BF16), pltpu.VMEM((D, F), BF16), pltpu.VMEM((D, F), BF16),
         pltpu.VMEM((B, D), BF16), pltpu.VMEM((B, F), BF16), pltpu.VMEM((B, F), BF16),
         pltpu.VMEM((B, F), BF16), pltpu.VMEM((B, F), BF16), pltpu.VMEM((B, F), BF16),
-        pltpu.VMEM((2, B, TN), F32), pltpu.VMEM((2, B, TN), BF16),
-        pltpu.SemaphoreType.DMA((3,)), pltpu.SemaphoreType.DMA((2,)), pltpu.SemaphoreType.DMA,
-        pltpu.SemaphoreType.DMA((2,)), pltpu.SemaphoreType.DMA((3,)), pltpu.SemaphoreType.DMA((2,)), pltpu.SemaphoreType.DMA((2,)),
+        pltpu.VMEM((PAIR, B, TN), F32), pltpu.VMEM((PAIR, B, TN), BF16),
+        pltpu.SemaphoreType.DMA((3,)), pltpu.SemaphoreType.DMA((PAIR,)), pltpu.SemaphoreType.DMA,
+        pltpu.SemaphoreType.DMA((PAIR,)), pltpu.SemaphoreType.DMA((3,)), pltpu.SemaphoreType.DMA((PAIR,)), pltpu.SemaphoreType.DMA((PAIR,)),
     )
 
     def second(hid_v, dy_v, acc, out_v, h_sem, dy_sem, o_sem):
@@ -600,11 +619,11 @@
         def tile(i):
             nt, kc = i // depth, i % depth
             return pltpu.make_async_copy(
-                gdy.at[pl.ds(pl.multiple_of(kc * TK, 8), TK), pl.ds(pl.multiple_of(nt * TND, 128), TND)],
-                dy_v.at[i % 2], dy_sem.at[i % 2])
+                gdy.at[subs(kc * TK, TK), lanes(nt * TND, TND)],
+                dy_v.at[i % PAIR], dy_sem.at[i % PAIR])
 
         def result(nt):
-            return pltpu.make_async_copy(out_v, dwd.at[:, pl.ds(pl.multiple_of(nt * TND, 128), TND)], o_sem)
+            return pltpu.make_async_copy(out_v, dwd.at[:, lanes(nt * TND, TND)], o_sem)
 
         hidden = pltpu.make_async_copy(hids, hid_v, h_sem)
         hidden.start()
@@ -623,7 +642,7 @@
                 clear(acc)
 
             acc[...] += lax.dot_general(
-                hid_v[pl.ds(pl.multiple_of(kc * TK, 8), TK), :], dy_v[i % 2], (((0,), (0,)), ((), ())), preferred_element_type=F32)
+                hid_v[subs(kc * TK, TK), :], dy_v[i % PAIR], ROWS, preferred_element_type=F32)
 
             @pl.when(kc == depth - 1)
             def _():
@@ -649,21 +668,21 @@
 
     pl.run_scoped(
         second,
-        pltpu.VMEM((T, F), BF16), pltpu.VMEM((2, TK, TND), BF16), pltpu.VMEM((F, TND), F32), pltpu.VMEM((F, TND), BF16),
-        pltpu.SemaphoreType.DMA, pltpu.SemaphoreType.DMA((2,)), pltpu.SemaphoreType.DMA,
+        pltpu.VMEM((T, F), BF16), pltpu.VMEM((PAIR, TK, TND), BF16), pltpu.VMEM((F, TND), F32), pltpu.VMEM((F, TND), BF16),
+        pltpu.SemaphoreType.DMA, pltpu.SemaphoreType.DMA((PAIR,)), pltpu.SemaphoreType.DMA,
     )
 
     def third(d_v, x_v, out_v, d_sem, x_sem, o_sem):
         steps = D // TM
         per_tick = -(-steps // (N_END - B_END))
-        half = pl.ds(pl.multiple_of(y * 4 * B, 8), 4 * B)
+        half = subs(y * 4 * B, 4 * B)
         grads = [pltpu.make_async_copy(h.at[half], d_v.at[:, pl.ds(i * F, F)], d_sem.at[i]) for i, h in enumerate((dgs, dus))]
 
         def tile(i):
-            return pltpu.make_async_copy(gx.at[half, pl.ds(pl.multiple_of(i * TM, 128), TM)], x_v.at[i % 2], x_sem.at[i % 2])
+            return pltpu.make_async_copy(gx.at[half, lanes(i * TM, TM)], x_v.at[i % PAIR], x_sem.at[i % PAIR])
 
         def result(i):
-            return pltpu.make_async_copy(out_v.at[i % 2], part.at[pl.ds(pl.multiple_of(i * TM, 8), TM)], o_sem.at[i % 2])
+            return pltpu.make_async_copy(out_v.at[i % PAIR], part.at[subs(i * TM, TM)], o_sem.at[i % PAIR])
 
         def step(i):
             tile(i).wait()
@@ -676,7 +695,7 @@
             def _():
                 result(i - 2).wait()
 
-            out_v[i % 2] = lax.dot_general(x_v[i % 2], d_v[...], (((0,), (0,)), ((), ())), preferred_element_type=F32)
+            out_v[i % PAIR] = lax.dot_general(x_v[i % PAIR], d_v[...], ROWS, preferred_element_type=F32)
             result(i).start()
 
         for copy in grads:
@@ -702,8 +721,8 @@
 
     pl.run_scoped(
         third,
-        pltpu.VMEM((4 * B, 2 * F), BF16), pltpu.VMEM((2, 4 * B, TM), BF16), pltpu.VMEM((2, TM, 2 * F), F32),
-        pltpu.SemaphoreType.DMA((2,)), pltpu.SemaphoreType.DMA((2,)), pltpu.SemaphoreType.DMA((2,)),
+        pltpu.VMEM((4 * B, 2 * F), BF16), pltpu.VMEM((PAIR, 4 * B, TM), BF16), pltpu.VMEM((PAIR, TM, 2 * F), F32),
+        pltpu.SemaphoreType.DMA((PAIR,)), pltpu.SemaphoreType.DMA((PAIR,)), pltpu.SemaphoreType.DMA((PAIR,)),
     )
 
     @pl.loop(N_END, T_END)
@@ -714,18 +733,18 @@
     for t in range(T_END, T_END + KEEP):
         arrive_y(1, t)
         arrive_y(1, t, True)
-        for d in (0, 1):
+        for d in BOTH:
             pass_cut(d, t, True)
     for q in range(4):
-        wait_sibling(1, (1 - y) * 4 + q)
-    for a in (0, 1):
+        wait_sibling(1, opp * 4 + q)
+    for a in BOTH:
         own_to_sibling(a).wait_send()
 
 
 def finish_kernel(dims, part, gx, dgs, dus, down, dwg, dwu, dwd, d_v, x_v, p_v, out_v, down_v, d_sem, x_sem, p_sem, o_sem, c_sem):
     R, D, F, TM = dims[0], dims[1], dims[2], dims[5]
     steps, depth = D // TM, gx.shape[0] // 2
-    half = pl.ds(pl.multiple_of((1 - lax.axis_index("tp") // 8) * depth, 8), depth)
+    half = subs((1 - lax.axis_index("tp") // 8) * depth, depth)
     grads = [pltpu.make_async_copy(h.at[half], d_v.at[:, pl.ds(i * F, F)], d_sem.at[i]) for i, h in enumerate((dgs, dus))]
     pieces, high = 8, F // 8
 
@@ -737,11 +756,11 @@
         ]
 
     def results(i):
-        at = pl.ds(pl.multiple_of(i * TM, 8), TM)
-        return [pltpu.make_async_copy(out_v.at[i % 2, n], h.at[at], o_sem.at[i % 2, n]) for n, h in enumerate((dwg, dwu))]
+        at = subs(i * TM, TM)
+        return [pltpu.make_async_copy(out_v.at[i % PAIR, n], h.at[at], o_sem.at[i % PAIR, n]) for n, h in enumerate((dwg, dwu))]
 
     def piece(way, i):
-        at = pl.ds(pl.multiple_of(i * high, 8), high)
+        at = subs(i * high, high)
         if way == 0:
             return pltpu.make_async_copy(down.at[at], down_v.at[at], c_sem.at[0, i])
         return pltpu.make_async_copy(down_v.at[at], dwd.at[at], c_sem.at[1, i])
@@ -775,9 +794,9 @@
             for copy in results(i - 2):
                 copy.wait()
 
-        total = p_v[i % 3] + lax.dot_general(x_v[i % 3], d_v[...], (((0,), (0,)), ((), ())), preferred_element_type=F32)
-        for n in (0, 1):
-            out_v[i % 2, n] = total[:, n * F : (n + 1) * F].astype(BF16)
+        total = p_v[i % 3] + lax.dot_general(x_v[i % 3], d_v[...], ROWS, preferred_element_type=F32)
+        for n in BOTH:
+            out_v[i % PAIR, n] = total[:, n * F : (n + 1) * F].astype(BF16)
         for copy in results(i):
             copy.start()
 
@@ -799,25 +818,26 @@
         shape((2, 6 * R, D), BF16), shape((T, F), BF16), shape((T, F), BF16), shape((T, F), BF16),
     )
     product = 2 * T * D * F
-    ysum, mysum, next_sum, back_sum, down, part, gx, _, _, _, _, dgs, dus, _ = pl.pallas_call(
+    ysum, mysum, pair_sum, inner_sum, down, part, gx, _, _, _, _, dgs, dus, _ = pl.pallas_call(
         functools.partial(kernel, dims),
         out_shape=outs,
         in_specs=[hbm] * 7,
         out_specs=[hbm] * len(outs),
         scratch_shapes=[
             vmem((3, C, D), F32), vmem((3, C, D), BF16), vmem((3, 2, C, D), BF16), vmem((3, 3, C, D), BF16),
-            dma((2, 2, 4)), dma((2, 2, 12)), dma((2, 4)), dma((2, 16)), dma((2,)), dma((3, 2, 4)), dma((2, 8)), dma((2,)), dma((2,)),
-            dma((2, 3)), dma((2, 3)), dma((2, 3)),
-            dma((2, 3)), dma((2, 24)), dma((BLOCKS,)), dma((3, 4)), dma,
+            dma((PAIR, PAIR, 4)), dma((PAIR, PAIR, 12)), dma((PAIR, 4)), dma((PAIR, 16)), dma((PAIR,)), dma((3, 2, 4)), dma((PAIR, 8)), dma((PAIR,)), dma((PAIR,)),
+            dma((PAIR, 3)), dma((PAIR, 3)), dma((PAIR, 3)),
+            dma((PAIR, 3)), dma((PAIR, 24)), dma((BLOCKS,)), dma((3, 4)), dma,
         ],
         compiler_params=pltpu.CompilerParams(collective_id=0, has_side_effects=True, vmem_limit_bytes=67043328),
         cost_estimate=pl.CostEstimate(flops=5 * product, bytes_accessed=10 * T * D, transcendentals=0),
         name="mlp_backward",
     )(x, dy, gate, up, wg, wu, wd)
+    around, spots = range(16), [i // 2 % 4 for i in range(16)]
     sums = [
-        lax.ppermute(ysum, "tp", [(i, (i + 8) % 16) for i in range(16)]),
-        lax.ppermute(next_sum, "tp", [(i, i + 2) for i in range(16) if i // 2 % 4 < 3]),
-        lax.ppermute(back_sum, "tp", [(i, i - 2) for i in range(16) if i // 2 % 4 > 0]),
+        lax.ppermute(ysum, "tp", [(i, (i + 8) % 16) for i in around]),
+        lax.ppermute(pair_sum, "tp", [(i, i ^ 2) for i in around]),
+        lax.ppermute(inner_sum, "tp", [(i, i + 2 if spots[i] == 1 else i - 2) for i in around if 0 < spots[i] < 3]),
     ]
     weights = pl.pallas_call(
         functools.partial(finish_kernel, dims),
@@ -825,8 +845,8 @@
         in_specs=[hbm] * 5,
         out_specs=[hbm] * 3,
         scratch_shapes=[
-            vmem((T // 2, 2 * F), BF16), vmem((3, T // 2, TM), BF16), vmem((3, TM, 2 * F), F32), vmem((2, 2, TM, F), BF16),
-            vmem((F, D), BF16), dma((2,)), dma((3,)), dma((3,)), dma((2, 2)), dma((2, 8)),
+            vmem((T // 2, 2 * F), BF16), vmem((3, T // 2, TM), BF16), vmem((3, TM, 2 * F), F32), vmem((PAIR, 2, TM, F), BF16),
+            vmem((F, D), BF16), dma((PAIR,)), dma((3,)), dma((3,)), dma((PAIR, 2)), dma((PAIR, 8)),
         ],
         compiler_params=pltpu.CompilerParams(vmem_limit_bytes=67043328),
         cost_estimate=pl.CostEstimate(flops=product, bytes_accessed=6 * T * D, transcendentals=0),

time: 455 us -> 449 us (0.987)
  transfers between devices with their start and end apart: 3 -> 3, of which waited for: 1 -> 0; matrix products, arithmetic and copies ran while one was open for 0% -> 0% of each run, Pallas kernels for 11% -> 11%
where the time goes in v4:
time: 449 us; the launch traced here: 448 us
  Pallas kernels  432 us (96%)
  starting transfers between devices  8.89 us (2%)
  other arithmetic  7.01 us (2%)
    pallas_call x1, Pallas kernels, fused(): pl.pallas_call(functools.partial(kernel, dims), out_shape=outs, in_specs=...  384 us
    pallas_call x1, Pallas kernels, fused(): pl.pallas_call(functools.partial(finish_kernel, dims), out_shape=(shape((...  48.2 us
  transfers between devices with their start and end apart: 3, of which 0 were waited for; matrix products, arithmetic and copies ran while one was open for 0% of the time, Pallas kernels for 11%

profile of v4, /device:TPU:0, one launch (start us, length us, event | category | flops | bytes accessed | tf_op | source)
XLA Modules:
  0.0 448.3 jit_solution(883635309438636631)
XLA Ops:
  0.6 383.5 %mlp_backward.1 = (bf16[224,5120]{1,0:T(8,128)(2,1)}, f32[224,5120]{1,0:T(8,128)}, bf16[224,5120]{1,0:T(8,128)(2,1)}, bf16[224,5120]{1,0:T(8,128)(2,1)}, bf16[10...) custom-call(bf16[224,5120]{1,0:T(8,128)(2,1)} %x.1, ...), custom_call_target="tpu_custom_call" | custom-call | flops 187904819200 | bytes 183500800 | tf_op jit(solution)/shard_map/mlp_backward/pallas_call | solution.py:821
  384.2 1.6 collective-permute-start
  385.7 5.2 %collective-permute-start.1 = (bf16[224,5120]{1,0:T(8,128)(2,1)}, bf16[224,5120]{1,0:T(8,128)(2,1)}, u32[]{:S(2)}, u32[]{:S(2)}) collective-permute-start(bf16[224,5120]{1,0:T(8,128)(2,1)} %get-tuple-element.18), channel_id=1, source_target_pairs={{0,2},{1,3},{2,0},{3,1},{4,6},{5,7},{6,4},{7,5},{8,10},{9,11},{10,... | collective-permute-start | bytes 6881288 | tf_op jit(solution)/shard_map/ppermute | solution.py:839
  391.0 2.1 collective-permute-start.2
  393.1 48.2 %finish.1 = (bf16[5120,1024]{1,0:T(8,128)(2,1)}, bf16[5120,1024]{1,0:T(8,128)(2,1)}, bf16[1024,5120]{1,0:T(8,128)(2,1)}) custom-call(f32[5120,2048]{1,0:T(8,128)} %get-tuple-element.20.part, bf16[3584,5120]{1,0:T(8,128)(2,1)} %get-tuple-element.21.gx, bf16[3584,1024]{1,0:T(8,128)(2,1)} %get-tuple-element.22.dgs, bf16[3584,1024]{1,0:T(8,128)(2,1)} %get-tuple-element.23.dus, ...), custom_call_target="tpu_custom_call" | custom-call | flops 37580963840 | bytes 110100480 | tf_op jit(solution)/shard_map/finish/pallas_call | solution.py:842
  441.2 0.0 collective-permute-done
  441.2 0.0 collective-permute-done.1
  441.3 0.0 collective-permute-done.2
  441.3 7.0 %add_convert_fusion = bf16[224,5120]{1,0:T(8,128)(2,1)} fusion(bf16[224,5120]{1,0:T(8,128)(2,1)} %collective-permute-done.2, bf16[224,5120]{1,0:T(8,128)(2,1)} %collective-permute-done.1, f32[224,5120]{1,0:T(8,128)} %get-tuple-element.16, bf16[224,5120]{1,0:T(8,128)(2,1)} %collective-permute-done), kind=kLoop, calls=%fused_computation | loop fusion | flops 8028160 | bytes 13762560 | tf_op jit(solution)/shard_map/convert_element_type | solution.py:855
Async XLA Ops:
  384.2 57.1 %collective-permute-start = (bf16[224,5120]{1,0:T(8,128)(2,1)}, bf16[224,5120]{1,0:T(8,128)(2,1)}, u32[]{:S(2)}, u32[]{:S(2)}) collective-permute-start(bf16[224,5120]{1,0:T(8,128)(2,1)} %get-tuple-element.17), channel_id=1, source_target_pairs={{0,8},{1,9},{2,10},{3,11},{4,12},{5,13},{6,14},{7,15},{8,0},{9,1},... | collective-permute-start | bytes 6881288 | tf_op jit(solution)/shard_map/ppermute | solution.py:838
  385.7 55.5 %collective-permute-start.1 = (bf16[224,5120]{1,0:T(8,128)(2,1)}, bf16[224,5120]{1,0:T(8,128)(2,1)}, u32[]{:S(2)}, u32[]{:S(2)}) collective-permute-start(bf16[224,5120]{1,0:T(8,128)(2,1)} %get-tuple-element.18), channel_id=1, source_target_pairs={{0,2},{1,3},{2,0},{3,1},{4,6},{5,7},{6,4},{7,5},{8,10},{9,11},{10,... | collective-permute-start | bytes 6881288 | tf_op jit(solution)/shard_map/ppermute | solution.py:839
  391.0 50.3 %collective-permute-start.2 = (bf16[224,5120]{1,0:T(8,128)(2,1)}, bf16[224,5120]{1,0:T(8,128)(2,1)}, u32[]{:S(2)}, u32[]{:S(2)}) collective-permute-start(bf16[224,5120]{1,0:T(8,128)(2,1)} %get-tuple-element.19), channel_id=1, source_target_pairs={{2,4},{3,5},{4,2},{5,3},{10,12},{11,13},{12,10},{13,11},{18,20},{1... | collective-permute-start | bytes 6881288 | tf_op jit(solution)/shard_map/ppermute | solution.py:840
